TPU v7x, 32 devices: a whole 2x2x4 slice. The times are simulated.
32 devices in a mesh: data: 32 (over z, y, x, core).
Axes of the slice: x: 2, y: 2, z: 4, core: 2. Of those that a mesh axis runs over, the one named last changes fastest.
Arguments:
- x_act: bfloat16 [256, 196, 512], P('data')
- y_tgt: bfloat16 [256, 196, 512], P('data')
- w_in: float32 [4, 512, 2048], replicated
- w_out: float32 [4, 2048, 512], replicated
Outputs:
- output 1: float32 [4, 512, 2048], replicated
- output 2: float32 [4, 2048, 512], replicated
- output 3: float32 [], replicated
All inputs are finite; a program needn't handle non-finite values.
Results may differ from a plain program's by a relative error of at most 0.00183218.
Values are sent between devices in bfloat16 or wider.
A program may use at most 1 GiB of HBM per device.

v0:
```python
import math
import jax
import jax.numpy as jnp
from jax import lax
from jax.sharding import PartitionSpec as P

RHO_FRAC = 0.1
LEARN_RATE = 1.0
MICRO_STEPS = 2


def gelu_tanh(z_val):
    return jax.nn.gelu(z_val, approximate=True)


def layer_forward(h_act, wi_cast, wo_cast):
    z_pre = jnp.einsum("bsd,df->bsf", h_act, wi_cast, preferred_element_type=jnp.float32).astype(jnp.bfloat16)
    gelu_out = gelu_tanh(z_pre.astype(jnp.float32)).astype(jnp.bfloat16)
    u_out = jnp.einsum("bsf,fd->bsd", gelu_out, wo_cast, preferred_element_type=jnp.float32)
    return (h_act.astype(jnp.float32) + u_out).astype(jnp.bfloat16), z_pre


def micro_grads(x_mb, y_mb, wi_list, wo_list):
    n_layers = len(wi_list)
    h_list = [x_mb]
    z_list = []
    for layer_idx in range(n_layers):
        h_next, z_pre = layer_forward(h_list[-1], wi_list[layer_idx], wo_list[layer_idx])
        h_list.append(h_next)
        z_list.append(z_pre)
    out_err = h_list[-1].astype(jnp.float32) - y_mb.astype(jnp.float32)
    sq_sum = jnp.sum(out_err * out_err)
    back_grad = out_err.astype(jnp.bfloat16)
    sums_in = [None] * n_layers
    sums_out = [None] * n_layers
    for layer_idx in reversed(range(n_layers)):
        gelu_out, gelu_vjp = jax.vjp(gelu_tanh, z_list[layer_idx].astype(jnp.float32))
        sums_out[layer_idx] = jnp.einsum("bsf,bsd->fd", gelu_out.astype(jnp.bfloat16), back_grad, preferred_element_type=jnp.float32)
        d_act = jnp.einsum("bsd,fd->bsf", back_grad, wo_list[layer_idx], preferred_element_type=jnp.float32)
        d_pre = gelu_vjp(d_act)[0].astype(jnp.bfloat16)
        sums_in[layer_idx] = jnp.einsum("bsd,bsf->df", h_list[layer_idx], d_pre, preferred_element_type=jnp.float32)
        if layer_idx > 0:
            back_in = jnp.einsum("bsf,df->bsd", d_pre, wi_list[layer_idx], preferred_element_type=jnp.float32)
            back_grad = (back_grad.astype(jnp.float32) + back_in).astype(jnp.bfloat16)
    return sums_in, sums_out, sq_sum


def grad_pass(x_loc, y_loc, wi_list, wo_list):
    mb_rows = x_loc.shape[0] // MICRO_STEPS
    sums_in, sums_out, sq_sum = micro_grads(x_loc[:mb_rows], y_loc[:mb_rows], wi_list, wo_list)
    for micro_idx in range(1, MICRO_STEPS):
        row_lo = micro_idx * mb_rows
        more_in, more_out, more_sq = micro_grads(x_loc[row_lo:row_lo + mb_rows], y_loc[row_lo:row_lo + mb_rows], wi_list, wo_list)
        sums_in = [left_sum + right_sum for left_sum, right_sum in zip(sums_in, more_in)]
        sums_out = [left_sum + right_sum for left_sum, right_sum in zip(sums_out, more_out)]
        sq_sum = sq_sum + more_sq
    return sums_in, sums_out, sq_sum


def solution(mesh):
    n_dev = mesh.shape["data"]

    def local_step(x_loc, y_loc, w_in, w_out):
        n_layers, d_model, d_ff = w_in.shape
        tok_scale = 1.0 / (x_loc.shape[0] * n_dev * x_loc.shape[1] * d_model)
        rho_val = RHO_FRAC * math.sqrt(n_layers * (d_model + d_ff))
        wi_cast = [w_in[layer_idx].astype(jnp.bfloat16) for layer_idx in range(n_layers)]
        wo_cast = [w_out[layer_idx].astype(jnp.bfloat16) for layer_idx in range(n_layers)]
        sums_in, sums_out, _ = grad_pass(x_loc, y_loc, wi_cast, wo_cast)
        grad_in = [lax.psum(part_sum, "data") * tok_scale for part_sum in sums_in]
        grad_out = [lax.psum(part_sum, "data") * tok_scale for part_sum in sums_out]
        sq_norm = sum(jnp.sum(grad_mat * grad_mat) for grad_mat in grad_in + grad_out)
        perturb_coef = rho_val / jnp.sqrt(sq_norm)
        pi_cast = [(w_in[layer_idx] + perturb_coef * grad_in[layer_idx]).astype(jnp.bfloat16) for layer_idx in range(n_layers)]
        po_cast = [(w_out[layer_idx] + perturb_coef * grad_out[layer_idx]).astype(jnp.bfloat16) for layer_idx in range(n_layers)]
        second_in, second_out, second_sq = grad_pass(x_loc, y_loc, pi_cast, po_cast)
        total_in = [lax.psum(part_sum, "data") for part_sum in second_in]
        total_out = [lax.psum(part_sum, "data") for part_sum in second_out]
        total_sq = lax.psum(second_sq, "data")
        new_in = jnp.stack([w_in[layer_idx] - LEARN_RATE * (total_in[layer_idx] * tok_scale) for layer_idx in range(n_layers)])
        new_out = jnp.stack([w_out[layer_idx] - LEARN_RATE * (total_out[layer_idx] * tok_scale) for layer_idx in range(n_layers)])
        pert_loss = 0.5 * (total_sq * tok_scale)
        return new_in, new_out, pert_loss

    return jax.shard_map(local_step, mesh=mesh, in_specs=(P("data"), P("data"), P(), P()), out_specs=(P(), P(), P()), check_vma=False)
```

profile of v0, /device:TPU:0, one launch (start us, length us, event | category | flops | bytes accessed | tf_op | source)
XLA Modules:
  0.0 1521.0 jit_solution(2168835752083281108)
XLA Ops:
  25.9 7.5 fusion.209
  85.8 5.9 fusion.66
  109.4 10.7 fusion.178
  141.7 5.9 fusion.48
  165.8 5.9 bitcast_add_fusion.9
  202.3 11.2 fusion.161
  213.6 501.1 %all-reduce.7.cloned.1.call-done = (f32[2048,512]{1,0:T(8,128)}, f32[512,2048]{1,0:T(8,128)}, f32[512,2048]{1,0:T(8,128)}, f32[512,2048]{1,0:T(8,128)}, f32[512,...) async-done(((f32[2048,512]{1,0:T(8,128)}, f32[512,2048]{1,0:T(8,128)}, f32[512,2048]{1,0:T(8,128)}, f32[512,2048]{1,0:T(8,128)}, ...) | async-done | bytes 33554448 | tf_op jit(solution)/shard_map/psum | solution.py:71
  738.0 16.2 %fusion.210 = (bf16[512,2048,1]{1,0,2:T(8,128)(2,1)}, bf16[512,2048,1]{1,0,2:T(8,128)(2,1)}, bf16[512,2048,1]{1,0,2:T(8,128)(2,1)}, bf16[512,2048,1]{1,0,2:T(8,128)(2,1)}) fusion(f32[512,2048]{1,0:T(8,128)} %get-tuple-element.15, f32[4,512,2048]{2,1,0:T(8,128)} %param.6, f32[]{:T(128)S(6)} %mul.931, f32[512,2048]{1,0:T(8,128)} %get-tuple-element.12, ...), kind=kLoop, calls=%fused_computation.342 | loop fusion | flops 12582912 | bytes 41943044 | tf_op jit(solution)/shard_map/convert_element_type | solution.py:74
  755.2 11.3 fusion.212
  796.5 6.2 fusion.275
  807.0 7.1 fusion.42
  860.3 7.0 fusion.30
  869.2 9.2 bitcast_add_fusion
  900.6 5.9 fusion.36
  919.3 11.2 fusion.182
  930.5 7.9 fusion.272
  938.4 10.8 fusion.160
  949.2 9.2 bitcast_add_fusion.3
  959.7 40.6 %psum.135 = f32[]{:T(128)} all-reduce(f32[]{:T(128)S(6)} %add.457), channel_id=1, replica_groups=mesh['data'=32] {'data'}, use_global_device_ids=true, to_apply=%region_26.0 | all-reduce | flops 1 | bytes 8 | tf_op jit(solution)/shard_map/psum | solution.py:79
  1001.0 456.1 %all-reduce.5.cloned.1.call-done = (f32[512,2048]{1,0:T(8,128)}, f32[512,2048]{1,0:T(8,128)}, f32[512,2048]{1,0:T(8,128)}, f32[512,2048]{1,0:T(8,128)}, f32[2048...) async-done(((f32[512,2048]{1,0:T(8,128)}, f32[512,2048]{1,0:T(8,128)}, f32[512,2048]{1,0:T(8,128)}, f32[512,2048]{1,0:T(8,128)}, ...) | async-done | bytes 33554448 | tf_op jit(solution)/shard_map/psum | solution.py:77
  1457.1 17.2 %fusion.177 = (f32[1,512,2048]{2,1,0:T(8,128)S(1)}, f32[1,512,2048]{2,1,0:T(8,128)}, f32[1,512,2048]{2,1,0:T(8,128)}, f32[1,512,2048]{2,1,0:T(8,128)}) fusion(f32[512,2048]{1,0:T(8,128)} %get-tuple-element.6, f32[4,512,2048]{2,1,0:T(8,128)} %param.6, f32[512,2048]{1,0:T(8,128)} %get-tuple-element.5, f32[512,2048]{1,0:T(8,128)} %get-tuple-element.4, ...), kind=kLoop, calls=%fused_computation.297 | loop fusion | flops 8388608 | bytes 50331648 | tf_op jit(solution)/shard_map/stack | solution.py:80
  1474.3 10.7 pad_maximum_fusion
  1485.0 17.1 %fusion.175 = (f32[1,2048,512]{2,1,0:T(8,128)S(1)}, f32[1,2048,512]{2,1,0:T(8,128)}, f32[1,2048,512]{2,1,0:T(8,128)}, f32[1,2048,512]{2,1,0:T(8,128)}) fusion(f32[2048,512]{1,0:T(8,128)} %get-tuple-element.10, f32[4,2048,512]{2,1,0:T(8,128)} %param.7, f32[2048,512]{1,0:T(8,128)} %get-tuple-element.9, f32[2048,512]{1,0:T(8,128)} %get-tuple-element.8, ...), kind=kLoop, calls=%fused_computation.292 | loop fusion | flops 8388608 | bytes 50331648 | tf_op jit(solution)/shard_map/stack | solution.py:81
  1502.1 10.7 pad_maximum_fusion.1
  (205 shorter events, 294.6 us)
Async XLA Ops:
  7.2 707.6 %all-reduce.7.cloned.1.call-start = ((), (), s32[]{:S(2)}) async-start(), calls=%async_computation.1 | async-start | bytes 67108864 | tf_op jit(solution)/shard_map/psum | solution.py:71
  10.7 98.7 %copy-start.29 = (bf16[4,196,512]{2,0,1:T(4,128)(2,1)}, bf16[4,196,512]{2,0,1:T(4,128)(2,1)S(1)}, u32[]{:S(2)}) copy-start(bf16[4,196,512]{2,0,1:T(4,128)(2,1)S(1)} %get-tuple-element.45) | copy-start | bytes 2408452
  20.3 35.7 %copy-start.18 = (bf16[512,2048,1]{1,0,2:T(8,128)(2,1)}, bf16[512,2048,1]{1,0,2:T(8,128)(2,1)S(1)}, u32[]{:S(2)}) copy-start(bf16[512,2048,1]{1,0,2:T(8,128)(2,1)S(1)} %get-tuple-element.35) | copy-start | bytes 6291460
  20.3 53.5 %copy-start.16 = (bf16[512,2048,1]{1,0,2:T(8,128)(2,1)}, bf16[512,2048,1]{1,0,2:T(8,128)(2,1)S(1)}, u32[]{:S(2)}) copy-start(bf16[512,2048,1]{1,0,2:T(8,128)(2,1)S(1)} %get-tuple-element.37) | copy-start | bytes 6291460
  25.9 77.8 %copy-start.39 = (bf16[4,196,2048]{2,1,0:T(8,128)(2,1)}, bf16[4,196,2048]{2,1,0:T(8,128)(2,1)S(1)}, u32[]{:S(2)}) copy-start(bf16[4,196,2048]{2,1,0:T(8,128)(2,1)S(1)} %convolution_convert_fusion.15) | copy-start | bytes 9633796
  33.5 16.8 %copy-start.27 = (bf16[2048,512,1]{1,0,2:T(8,128)(2,1)}, bf16[2048,512,1]{1,0,2:T(8,128)(2,1)S(1)}, u32[]{:S(2)}) copy-start(bf16[2048,512,1]{1,0,2:T(8,128)(2,1)S(1)} %get-tuple-element.41) | copy-start | bytes 6291460
  33.5 34.6 %copy-start.25 = (bf16[2048,512,1]{1,0,2:T(8,128)(2,1)}, bf16[2048,512,1]{1,0,2:T(8,128)(2,1)S(1)}, u32[]{:S(2)}) copy-start(bf16[2048,512,1]{1,0,2:T(8,128)(2,1)S(1)} %get-tuple-element.38) | copy-start | bytes 6291460
  33.5 52.3 %copy-start.23 = (bf16[2048,512,1]{1,0,2:T(8,128)(2,1)}, bf16[2048,512,1]{1,0,2:T(8,128)(2,1)S(1)}, u32[]{:S(2)}) copy-start(bf16[2048,512,1]{1,0,2:T(8,128)(2,1)S(1)} %get-tuple-element.39) | copy-start | bytes 6291460
  93.7 10.1 copy-start.53
  124.6 72.1 %copy-start.38 = (bf16[4,196,2048]{2,1,0:T(8,128)(2,1)}, bf16[4,196,2048]{2,1,0:T(8,128)(2,1)S(1)}, u32[]{:S(2)}) copy-start(bf16[4,196,2048]{2,1,0:T(8,128)(2,1)S(1)} %convolution_convert_fusion.11) | copy-start | bytes 9633796
  160.1 5.7 copy-start.58
  186.3 10.3 copy-start.52
  190.9 5.7 copy-start.54
  196.6 5.7 copy-start.22
  213.6 1243.5 %all-reduce.5.cloned.1.call-start = ((), (), s32[]{:S(2)}) async-start(), calls=%async_computation | async-start | bytes 67108864 | tf_op jit(solution)/shard_map/psum | solution.py:77
  714.7 5.9 copy-start.7
  737.9 16.2 %copy-start.3 = (f32[2048,512]{1,0:T(8,128)S(1)}, f32[2048,512]{1,0:T(8,128)}, u32[]{:S(2)}) copy-start(f32[2048,512]{1,0:T(8,128)} %get-tuple-element.11) | copy-start | bytes 12582916
  737.9 16.2 %copy-start.4 = (f32[2048,512]{1,0:T(8,128)S(1)}, f32[2048,512]{1,0:T(8,128)}, u32[]{:S(2)}) copy-start(f32[2048,512]{1,0:T(8,128)} %get-tuple-element.16) | copy-start | bytes 12582916
  737.9 17.3 %copy-start.5 = (f32[2048,512]{1,0:T(8,128)S(1)}, f32[2048,512]{1,0:T(8,128)}, u32[]{:S(2)}) copy-start(f32[2048,512]{1,0:T(8,128)} %get-tuple-element.17) | copy-start | bytes 12582916
  770.4 70.2 %copy-start.40 = (bf16[2048,4,196]{0,2,1:T(8,128)(2,1)}, bf16[2048,4,196]{0,2,1:T(8,128)(2,1)S(1)}, u32[]{:S(2)}) copy-start(bf16[2048,4,196]{0,2,1:T(8,128)(2,1)S(1)} %convolution_convert_fusion.3) | copy-start | bytes 9633796
  818.5 5.6 copy-start.45
  835.0 5.6 copy-start.33
  882.9 5.7 copy-start.59
  930.5 7.9 copy-start.31
  (38 other events, 112.6 us)
Sparse Core Ops, SparseCore 0:
  213.7 501.0 all-reduce.6
  958.5 498.4 all-reduce.4
where the time goes:
time: 1520 us
  waiting for transfers between devices  957 us (63%)
  matrix products  373 us (25%)
  other arithmetic  101 us (7%)
  blocking collectives  40.6 us (3%)
  local copies, waits for them, and re-layouts  25.8 us (2%)
  between operations  23.7 us (2%)
    psum x1, waiting for transfers between devices, local_step(): grad_out = [lax.psum(part_sum, 'data') * tok_scale for part_sum in sums_out]  501 us
    psum x1, waiting for transfers between devices, local_step(): total_in = [lax.psum(part_sum, 'data') for part_sum in second_in]  456 us
    dot_general x16, matrix products, micro_grads(): jnp.einsum('bsf,bsd->fd', gelu_out.astype(jnp.bfloat16), back_grad, prefe...  100 us
    dot_general x16, matrix products, micro_grads(): jnp.einsum('bsd,bsf->df', h_list[layer_idx], d_pre, preferred_element_typ...  91.1 us
    dot_general x12, matrix products, micro_grads(): jnp.einsum('bsd,fd->bsf', back_grad, wo_list[layer_idx], preferred_elemen...  71.5 us
    dot_general x16, matrix products, layer_forward(): jnp.einsum('bsf,fd->bsd', gelu_out, wo_cast, preferred_element_type=jnp.f...  46.9 us
    psum x1, blocking collectives, local_step(): total_sq = lax.psum(second_sq, 'data')  40.6 us
    dot_general x16, matrix products, layer_forward(): jnp.einsum('bsd,df->bsf', h_act, wi_cast, preferred_element_type=jnp.floa...  38.2 us
  transfers between devices with their start and end apart: 2, of which 2 were waited for; matrix products, arithmetic and copies ran while one was open for 0% of the time, Pallas kernels for 0%

commit v1 on v0

v1 whole, which is shorter than its diff:
```python
import functools
import math

import jax
import jax.numpy as jnp
from jax import lax
from jax.experimental import pallas as pl
from jax.experimental.pallas import tpu as pltpu
from jax.sharding import PartitionSpec as P

MESH = pl.DeviceIdType.MESH
F32 = jnp.float32

class Geo:
    pass

def geometry():
    g = Geo()
    me = lax.axis_index("data")
    g.me = me
    g.c = lax.rem(me, 2)
    g.x = lax.rem(me // 2, 2)
    g.y = lax.rem(me // 4, 2)
    g.z = me // 8
    g.partner = me + 1 - 2 * g.c
    g.xn = me + 2 - 4 * g.x
    g.yn = me + 4 - 8 * g.y
    g.zm = me - 8
    g.zp = me + 8
    g.sink = jnp.logical_or(g.z == 0, g.z == 3)
    g.e = g.z // 3
    return g

def entry_barrier(g):
    bar = pltpu.get_barrier_semaphore()
    for d in (g.partner, g.xn, g.yn):
        pl.semaphore_signal(bar, inc=1, device_id=(d,), device_id_type=MESH)
    @pl.when(g.z > 0)
    def _():
        pl.semaphore_signal(bar, inc=1, device_id=(g.zm,), device_id_type=MESH)
    @pl.when(g.z < 3)
    def _():
        pl.semaphore_signal(bar, inc=1, device_id=(g.zp,), device_id_type=MESH)
    @pl.when(g.sink)
    def _():
        pl.semaphore_wait(bar, 4)
    @pl.when(jnp.logical_not(g.sink))
    def _():
        pl.semaphore_wait(bar, 5)

FD, FX1, FY1, FMA, FMB, FPA, FPB, FY3, FX3 = range(9)
NFLOW = 9
CD, CX1, CY1, CM, CP, CY3, CX3 = range(7)
NCRED = 7
SHAPES = ((256, 512), (512, 256))

def rem(a, n):
    return lax.rem(a, n)

class RS:
    def __init__(self, g, n, ns, nsl, lags, bufs, own, sq=None):
        self.g, self.n, self.ns, self.nsl = g, n, ns, nsl
        self.LD, self.L1, self.LZ, self.L3 = lags
        (self.S, self.rD, self.r1, self.rz, self.r3, self.ssem, self.rsem, self.cred) = bufs
        self.own = own
        self.lam1 = self.LD
        self.lam2 = self.lam1 + self.L1
        self.lam3 = self.lam2 + 3 * self.LZ
        self.lam4 = self.lam3 + self.L3

    def copy(self, T, flow, k, src, dst, dev):
        slot = rem(k, self.ns)
        return pltpu.make_async_remote_copy(src_ref=src, dst_ref=dst,
            send_sem=self.ssem.at[T, flow, slot], recv_sem=self.rsem.at[T, flow, slot],
            device_id=(dev,), device_id_type=MESH)

    def take_credit(self, T, cr, k):
        @pl.when(k >= self.ns)
        def _():
            pl.semaphore_wait(self.cred.at[T, cr], 1)

    def give_credit(self, T, cr, k, dev):
        @pl.when(k + self.ns < self.n)
        def _():
            pl.semaphore_signal(self.cred.at[T, cr], inc=1, device_id=(dev,), device_id_type=MESH)

    def rows(self, T):
        R = SHAPES[T][0]
        g = self.g
        half = g.c * (R // 2)
        a, b = half, half + R // 4
        return R, half, a, b

    def ds(self, start, size):
        return pl.ds(pl.multiple_of(start, 8), size)

    def cD(self, T, k):
        R, half, a, b = self.rows(T)
        src = self.S[T].at[rem(k, self.nsl), self.ds((1 - self.g.c) * (R // 2), R // 2), :]
        return self.copy(T, FD, k, src, self.rD[T].at[rem(k, self.ns)], self.g.partner)

    def cX1(self, T, k):
        R, half, a, b = self.rows(T)
        src = self.S[T].at[rem(k, self.nsl), self.ds(a + (1 - self.g.x) * (R // 8), R // 8), :]
        return self.copy(T, FX1, k, src, self.r1[T].at[rem(k, self.ns), 0], self.g.xn)

    def cY1(self, T, k):
        R, half, a, b = self.rows(T)
        src = self.S[T].at[rem(k, self.nsl), self.ds(b + (1 - self.g.y) * (R // 8), R // 8), :]
        return self.copy(T, FY1, k, src, self.r1[T].at[rem(k, self.ns), 1], self.g.yn)

    def zpart(self, T, ab, e):
        R, half, a, b = self.rows(T)
        base = (a + self.g.x * (R // 8)) if ab == 0 else (b + self.g.y * (R // 8))
        return self.ds(base + e * (R // 16), R // 16)

    def cZ(self, T, k, dirn, ab):
        src = self.S[T].at[rem(k, self.nsl), self.zpart(T, ab, dirn), :]
        dst = self.rz[T].at[rem(k, self.ns), ab, dirn]
        flow = (FMA, FMB, FPA, FPB)[2 * dirn + ab]
        return self.copy(T, flow, k, src, dst, self.g.zp if dirn else self.g.zm)

    def fin(self, T, ab, mine):
        R, half, a, b = self.rows(T)
        g = self.g
        base = (a + g.x * (R // 8)) if ab == 0 else (b + g.y * (R // 8))
        base = base + g.e * (R // 16)
        w = g.y if ab == 0 else g.x
        w = w if mine else 1 - w
        if T == 0:
            return self.ds(base, 16), pl.ds(pl.multiple_of(w * 256, 256), 256)
        return self.ds(base + w * 16, 16), pl.ds(0, 256)

    def c3(self, T, k, ab):
        r, cc = self.fin(T, ab, False)
        src = self.S[T].at[rem(k, self.nsl), r, cc]
        dst = self.r3[T].at[rem(k, self.ns), ab]
        return self.copy(T, FY3 if ab == 0 else FX3, k, src, dst, self.g.yn if ab == 0 else self.g.xn)

    def h0(self, T, k):
        self.take_credit(T, CD, k)
        self.cD(T, k).start()

    def h1(self, T, k):
        R, half, a, b = self.rows(T)
        c = self.cD(T, k)
        c.wait()
        s, q = rem(k, self.nsl), rem(k, self.ns)
        h = self.ds(half, R // 2)
        self.S[T][s, h, :] = self.S[T][s, h, :] + self.rD[T][q]
        self.give_credit(T, CD, k, self.g.partner)
        self.take_credit(T, CX1, k)
        self.cX1(T, k).start()
        self.take_credit(T, CY1, k)
        self.cY1(T, k).start()

    def h2(self, T, k):
        R, half, a, b = self.rows(T)
        self.cX1(T, k).wait()
        self.cY1(T, k).wait()
        s, q = rem(k, self.nsl), rem(k, self.ns)
        ra = self.ds(a + self.g.x * (R // 8), R // 8)
        rb = self.ds(b + self.g.y * (R // 8), R // 8)
        self.S[T][s, ra, :] = self.S[T][s, ra, :] + self.r1[T][q, 0]
        self.S[T][s, rb, :] = self.S[T][s, rb, :] + self.r1[T][q, 1]
        self.give_credit(T, CX1, k, self.g.xn)
        self.give_credit(T, CY1, k, self.g.yn)

    def hz(self, T, k, dirn):
        g = self.g
        p = g.z if dirn else 3 - g.z
        s, q = rem(k, self.nsl), rem(k, self.ns)
        cr = CP if dirn else CM
        up = g.zm if dirn else g.zp
        @pl.when(k < self.n)
        def _():
            @pl.when(p > 0)
            def _():
                for ab in (0, 1):
                    self.cZ(T, k, dirn, ab).wait_recv()
                for ab in (0, 1):
                    r = self.zpart(T, ab, dirn)
                    self.S[T][s, r, :] = self.S[T][s, r, :] + self.rz[T][q, ab, dirn]
                self.give_credit(T, cr, k, up)
            @pl.when(p < 3)
            def _():
                self.take_credit(T, cr, k)
                for ab in (0, 1):
                    self.cZ(T, k, dirn, ab).start()
            @pl.when(p == 3)
            def _():
                self.take_credit(T, CY3, k)
                self.c3(T, k, 0).start()
                self.take_credit(T, CX3, k)
                self.c3(T, k, 1).start()
        @pl.when(jnp.logical_and(k >= 1, p < 3))
        def _():
            for ab in (0, 1):
                self.cZ(T, k - 1, dirn, ab).wait_send()

    def h4(self, T, k):
        @pl.when(self.g.sink)
        def _():
            s, q = rem(k, self.nsl), rem(k, self.ns)
            for ab in (0, 1):
                self.c3(T, k, ab).wait()
            for ab in (0, 1):
                r, cc = self.fin(T, ab, True)
                self.own[T][k, ab] = self.S[T][s, r, cc] + self.r3[T][q, ab]
            self.give_credit(T, CY3, k, self.g.yn)
            self.give_credit(T, CX3, k, self.g.xn)

    def due(self, s, j, order):
        n = self.n
        def at(T, lam):
            d = j - T - lam
            return (s + d // 2) if d % 2 == 0 else None
        for what in order:
            for T in (0, 1):
                if what == 1:
                    k = at(T, self.lam1)
                    if k is not None:
                        pl.when(jnp.logical_and(k >= 0, k < n))(functools.partial(self.h1, T, k))
                elif what == 2:
                    k = at(T, self.lam2)
                    if k is not None:
                        pl.when(jnp.logical_and(k >= 0, k < n))(functools.partial(self.h2, T, k))
                        for dirn in (0, 1):
                            p = self.g.z if dirn else 3 - self.g.z
                            kz = k - p * (self.LZ // 2)
                            pl.when(jnp.logical_and(kz >= 0, kz <= n))(functools.partial(self.hz, T, kz, dirn))
                elif what == 4:
                    k = at(T, self.lam4)
                    if k is not None:
                        pl.when(jnp.logical_and(k >= 0, k < n))(functools.partial(self.h4, T, k))

    def n_ticks(self):
        last = 2 * (self.n - 1) + 1 + max(self.lam4, self.lam3 + 2)
        return last // 2 + 1

def rs_scratch(ns, nsl):
    out = []
    for T in (0, 1):
        R, C = SHAPES[T]
        out += [pltpu.VMEM((nsl, R, C), F32), pltpu.VMEM((ns, R // 2, C), F32), pltpu.VMEM((ns, 2, R // 8, C), F32),
                pltpu.VMEM((ns, 2, 2, R // 16, C), F32), pltpu.VMEM((ns, 2, 16, 256), F32)]
    out += [pltpu.SemaphoreType.DMA((2, NFLOW, ns)), pltpu.SemaphoreType.DMA((2, NFLOW, ns)), pltpu.SemaphoreType.REGULAR((2, NCRED))]
    return out

def unpack_scratch(refs):
    o, i = refs[0:5], refs[5:10]
    bufs = [[o[m], i[m]] for m in range(5)]
    return tuple(bufs) + tuple(refs[10:13])

def rs_only_kernel(n, ns, nsl, lags, nl, so_ref, si_ref, own_o, own_i, *scr):
    bufs = unpack_scratch(scr[:13])
    lsem = scr[13]
    g = geometry()
    entry_barrier(g)
    rs = RS(g, n, ns, nsl, lags, bufs, (own_o, own_i))
    def load(T, k):
        li, f = k // 8, rem(k, 8)
        if T == 0:
            src = so_ref.at[li, pl.ds(pl.multiple_of(f * 256, 256), 256), :]
        else:
            src = si_ref.at[li, :, pl.ds(pl.multiple_of(f * 256, 256), 256)]
        return pltpu.make_async_copy(src, bufs[0][T].at[rem(k, nsl)], lsem.at[T, rem(k, 2)])
    for T in (0, 1):
        load(T, 0).start()
    def body(s, _):
        for j in (0, 1):
            @pl.when(s < n)
            def _():
                load(j, s).wait()
                rs.h0(j, s)
                @pl.when(s + 1 < n)
                def _():
                    load(j, s + 1).start()
            rs.due(s, j, (4, 2, 1))
        return 0
    lax.fori_loop(0, rs.n_ticks(), body, 0)

def rs_only(so, si, ns=4, nsl=9, lags=(1, 2, 2, 2), cid=1):
    n = so.shape[0] * 8
    return pl.pallas_call(
        functools.partial(rs_only_kernel, n, ns, nsl, lags, so.shape[0]),
        out_shape=[jax.ShapeDtypeStruct((n, 2, 16, 256), F32)] * 2,
        in_specs=[pl.BlockSpec(memory_space=pl.ANY)] * 2,
        out_specs=[pl.BlockSpec(memory_space=pltpu.VMEM)] * 2,
        scratch_shapes=rs_scratch(ns, nsl) + [pltpu.SemaphoreType.DMA((2, 2))],
        compiler_params=pltpu.CompilerParams(collective_id=cid, has_side_effects=True, vmem_limit_bytes=60 * 2**20),
        name="rs_only",
    )(so, si)


GS3, GM, GP, GE0, GE1, GD = range(6)
NGF = 6

class AG:
    def __init__(self, g, n, lags, own, out, ssem, rsem, lsem, layer, ns):
        self.g, self.n, self.own, self.out = g, n, own, out
        self.ssem, self.rsem, self.lsem = ssem, rsem, lsem
        self.layer, self.ns = layer, ns
        self.G3, self.GZ, self.GE, self.GDL = lags
        self.m1 = self.G3
        self.m2 = self.m1 + 3 * self.GZ + self.GE
        self.m3 = self.m2 + self.GDL

    def region(self, T, k, row, nrow, col=None, ncol=None):
        li, f = self.layer(k // 8), rem(k, 8)
        f0 = f * 256
        if T == 0:
            c = slice(None) if col is None else pl.ds(pl.multiple_of(col, 256), ncol)
            return self.out[0].at[li, pl.ds(pl.multiple_of(f0 + row, 16), nrow), c]
        return self.out[1].at[li, pl.ds(pl.multiple_of(row, 16), nrow), pl.ds(pl.multiple_of(f0, 256), 256)]

    def base(self, T, ab, w):
        R = SHAPES[T][0]
        return self.g.c * (R // 2) + ab * (R // 4) + w * (R // 8)

    def piece(self, T, k, ab):
        R = SHAPES[T][0]
        g = self.g
        b = self.base(T, ab, g.x if ab == 0 else g.y) + g.e * (R // 16)
        w = g.y if ab == 0 else g.x
        if T == 0:
            return self.region(T, k, b, 16, w * 256, 256)
        return self.region(T, k, b + w * 16, 16)

    def zpart(self, T, k, ab, e):
        R = SHAPES[T][0]
        g = self.g
        return self.region(T, k, self.base(T, ab, g.x if ab == 0 else g.y) + e * (R // 16), R // 16)

    def rcopy(self, T, flow, k, src, dst, dev):
        return pltpu.make_async_remote_copy(src_ref=src, dst_ref=dst, send_sem=self.ssem.at[T, flow, rem(k, self.ns)],
            recv_sem=self.rsem.at[T, flow, k], device_id=(dev,), device_id_type=MESH)

    def wait2(self, sem, region):
        pltpu.make_async_copy(region, region, sem).wait()

    def pair(self, T, k):
        R = SHAPES[T][0]
        return self.region(T, k, 0, R // 8)

    def g0(self, T, k):
        g = self.g
        @pl.when(g.sink)
        def _():
            for ab in (0, 1):
                dst = self.piece(T, k, ab)
                src = self.own[T].at[k, ab]
                pltpu.make_async_copy(src, dst, self.lsem.at[T, ab, rem(k, self.ns)]).start()
                self.rcopy(T, GS3, k, src, dst, g.yn if ab == 0 else g.xn).start()

    def wait_s3(self, T, k):
        for ab in (0, 1):
            pltpu.make_async_copy(self.own[T].at[k, ab], self.piece(T, k, ab), self.lsem.at[T, ab, rem(k, self.ns)]).wait()
        two = self.own[T].at[k]
        self.wait2(self.ssem.at[T, GS3, rem(k, self.ns)], two)
        self.wait2(self.rsem.at[T, GS3, k], two)

    def gz(self, T, k, dirn):
        g = self.g
        e = 1 - dirn
        p = g.z if dirn else 3 - g.z
        fz = GP if dirn else GM
        fe = GE1 if e else GE0
        nxt = g.zp if dirn else g.zm
        @pl.when(k < self.n)
        def _():
            @pl.when(p == 0)
            def _():
                self.wait_s3(T, k)
            @pl.when(p > 0)
            def _():
                self.wait2(self.rsem.at[T, fz, k], self.pair(T, k))
            @pl.when(p < 3)
            def _():
                for ab in (0, 1):
                    r = self.zpart(T, k, ab, e)
                    self.rcopy(T, fz, k, r, r, nxt).start()
            for ab in (0, 1):
                r = self.zpart(T, k, ab, e)
                self.rcopy(T, fe, k, r, r, g.xn if ab == 0 else g.yn).start()
        @pl.when(jnp.logical_and(k >= 1, p < 3))
        def _():
            self.wait2(self.ssem.at[T, fz, rem(k - 1, self.ns)], self.pair(T, k - 1))

    def half(self, T, k, c):
        R = SHAPES[T][0]
        return self.region(T, k, c * (R // 2), R // 2)

    def g2(self, T, k):
        g = self.g
        for f in (GE0, GE1):
            self.wait2(self.ssem.at[T, f, rem(k, self.ns)], self.pair(T, k))
            self.wait2(self.rsem.at[T, f, k], self.pair(T, k))
        r = self.half(T, k, g.c)
        self.rcopy(T, GD, k, r, r, g.partner).start()

    def g3(self, T, k):
        r = self.half(T, k, self.g.c)
        self.rcopy(T, GD, k, r, r, self.g.partner).wait()

    def due(self, s, j):
        n = self.n
        def at(T, lam):
            d = j - T - lam
            return (s + d // 2) if d % 2 == 0 else None
        for T in (0, 1):
            k = at(T, 0)
            if k is not None:
                pl.when(jnp.logical_and(k >= 0, k < n))(functools.partial(self.g0, T, k))
        for T in (0, 1):
            k = at(T, self.m1)
            if k is not None:
                for dirn in (0, 1):
                    p = self.g.z if dirn else 3 - self.g.z
                    kz = k - p * (self.GZ // 2)
                    pl.when(jnp.logical_and(kz >= 0, kz <= n))(functools.partial(self.gz, T, kz, dirn))
        for T in (0, 1):
            k = at(T, self.m2)
            if k is not None:
                pl.when(jnp.logical_and(k >= 0, k < n))(functools.partial(self.g2, T, k))
            k = at(T, self.m3)
            if k is not None:
                pl.when(jnp.logical_and(k >= 0, k < n))(functools.partial(self.g3, T, k))

    def n_ticks(self):
        last = 2 * (self.n - 1) + 1 + max(self.m3, self.m1 + 3 * self.GZ + 2)
        return last // 2 + 1

def ag_scratch(n, ns, dtype):
    return [pltpu.VMEM((n, 2, 16, 256), dtype), pltpu.VMEM((n, 2, 16, 256), dtype),
            pltpu.SemaphoreType.DMA((2, NGF, ns)), pltpu.SemaphoreType.DMA((2, NGF, n)), pltpu.SemaphoreType.DMA((2, 2, ns))]

def ag_kernel(n, ns, lags, order, sc_ref, own_o, own_i, wo_ref, wi_ref, out_o, out_i, w_o, w_i, pe_o, pe_i, ssem, rsem, lsem, wsem):
    g = geometry()
    layer = lambda q: order[0] + order[1] * q
    ag = AG(g, n, lags, (pe_o, pe_i), (out_o, out_i), ssem, rsem, lsem, layer, ns)
    wag = AG(g, n, lags, (pe_o, pe_i), (wo_ref, wi_ref), ssem, rsem, lsem, layer, ns)
    entry_barrier(g)
    @pl.when(g.sink)
    def _():
        def issue(k, _):
            for T in (0, 1):
                for ab in (0, 1):
                    pltpu.make_async_copy(wag.piece(T, k, ab), (w_o, w_i)[T].at[k, ab], wsem.at[T]).start()
            return 0
        lax.fori_loop(0, n, issue, 0)
        pltpu.make_async_copy(w_o, w_o, wsem.at[0]).wait()
        pltpu.make_async_copy(w_i, w_i, wsem.at[1]).wait()
    a, b = sc_ref[0], sc_ref[1]
    def body(s, _):
        @pl.when(jnp.logical_and(g.sink, s < n))
        def _():
            for T in (0, 1):
                ow = (own_o, own_i)[T]
                (pe_o, pe_i)[T][s] = ((w_o, w_i)[T][s] + a * (ow[s] * b)).astype(pe_o.dtype)
        for j in (0, 1):
            ag.due(s, j)
        return 0
    lax.fori_loop(0, ag.n_ticks(), body, 0)

def ag_call(sc, own_o, own_i, wo, wi, dtype, order, ns=4, lags=(4, 4, 4, 2), cid=2):
    n = own_o.shape[0]
    L = wo.shape[0]
    vm = pl.BlockSpec(memory_space=pltpu.VMEM)
    anyspec = pl.BlockSpec(memory_space=pl.ANY)
    return pl.pallas_call(
        functools.partial(ag_kernel, n, ns, lags, order),
        out_shape=[jax.ShapeDtypeStruct(wo.shape, dtype), jax.ShapeDtypeStruct(wi.shape, dtype)],
        in_specs=[pl.BlockSpec(memory_space=pltpu.SMEM), vm, vm, anyspec, anyspec],
        out_specs=[anyspec, anyspec],
        scratch_shapes=[pltpu.VMEM((n, 2, 16, 256), F32)] * 2 + ag_scratch(n, ns, dtype) + [pltpu.SemaphoreType.DMA((2,))],
        compiler_params=pltpu.CompilerParams(collective_id=cid, has_side_effects=True, vmem_limit_bytes=40 * 2**20),
        name="gather",
    )(sc, own_o, own_i, wo, wi)


RHO_FRAC = 0.1
LEARN_RATE = 1.0
BF = jnp.bfloat16


def gelu_tanh(z_val):
    return jax.nn.gelu(z_val, approximate=True)


def dot(a, b, dims):
    return lax.dot_general(a, b, (dims, ((), ())), preferred_element_type=F32)


def forward(x, wi, wo):
    h, hs, zs = x, [x], []
    for layer in range(len(wi)):
        z = dot(h, wi[layer], ((1,), (0,))).astype(BF)
        a = gelu_tanh(z.astype(F32)).astype(BF)
        h = (h.astype(F32) + dot(a, wo[layer], ((1,), (0,)))).astype(BF)
        hs.append(h)
        zs.append(z)
    return hs, zs


def backward(hs, zs, q, wi, wo):
    n_layers = len(wi)
    s_in, s_out = [None] * n_layers, [None] * n_layers
    for layer in reversed(range(n_layers)):
        a, vjp = jax.vjp(gelu_tanh, zs[layer].astype(F32))
        s_out[layer] = dot(a.astype(BF), q, ((0,), (0,)))
        p = vjp(dot(q, wo[layer], ((1,), (1,))))[0].astype(BF)
        s_in[layer] = dot(hs[layer], p, ((0,), (0,)))
        if layer:
            q = (q.astype(F32) + dot(p, wi[layer], ((1,), (1,)))).astype(BF)
    return s_in, s_out


def solution(mesh):
    n_dev = mesh.shape["data"]

    def local_step(x_loc, y_loc, w_in, w_out):
        n_layers, d_model, d_ff = w_in.shape
        tok = 1.0 / (x_loc.shape[0] * n_dev * x_loc.shape[1] * d_model)
        rho = RHO_FRAC * math.sqrt(n_layers * (d_model + d_ff))
        x = x_loc.reshape(-1, d_model)
        y = y_loc.reshape(-1, d_model)
        sink = lax.rem(lax.axis_index("data") // 8, 3) == 0

        def one_pass(wi, wo, cid):
            hs, zs = forward(x, wi, wo)
            err = hs[-1].astype(F32) - y.astype(F32)
            s_in, s_out = backward(hs, zs, err.astype(BF), wi, wo)
            own_o, own_i = rs_only(jnp.stack(s_out), jnp.stack(s_in), lags=(1, 4, 4, 4), nsl=14, ns=4, cid=cid)
            return own_o, own_i, jnp.sum(err * err)

        wi = [w_in[k].astype(BF) for k in range(n_layers)]
        wo = [w_out[k].astype(BF) for k in range(n_layers)]
        own_o, own_i, _ = one_pass(wi, wo, 1)
        go, gi = own_o * tok, own_i * tok
        part = jnp.sum(go * go) + jnp.sum(gi * gi)
        sq = lax.psum(jnp.where(sink, part, 0.0), "data")
        coef = rho / jnp.sqrt(sq)
        sc = jnp.stack([coef, jnp.float32(tok)])
        vo, vi = ag_call(sc, own_o, own_i, w_out, w_in, BF, (0, 1), cid=2)
        wi = [vi[k] for k in range(n_layers)]
        wo = [vo[k] for k in range(n_layers)]
        own_o, own_i, sq2 = one_pass(wi, wo, 3)
        sc = jnp.array([-LEARN_RATE, tok], F32)
        new_out, new_in = ag_call(sc, own_o, own_i, w_out, w_in, F32, (0, 1), cid=4)
        loss = 0.5 * (lax.psum(sq2, "data") * tok)
        return new_in, new_out, loss

    return jax.shard_map(local_step, mesh=mesh, in_specs=(P("data"), P("data"), P(), P()), out_specs=(P(), P(), P()), check_vma=False)
```

time: 1520 us -> 1010 us (0.66)
  waiting for transfers between devices: 957 us -> 0 us
  Pallas kernels: 0 us -> 467 us
  other arithmetic: 101 us -> 48.1 us
  blocking collectives: 40.6 us -> 76.8 us
  local copies, waits for them, and re-layouts: 25.8 us -> 47.9 us
  matrix products: 373 us -> 353 us
  between operations: 23.7 us -> 5.54 us
    psum x2 -> x0, waiting for transfers between devices: 957 us -> none  [the longest x1 501 us: local_step(): grad_out = [lax.psum(part_sum, 'data') * tok_scale for part_sum in sums_out]]
    pallas_call x0 -> x4, Pallas kernels: none -> 467 us  [the longest x2 264 us: rs_only(): pl.pallas_call(functools.partial(rs_only_kernel, n, ns, nsl, lags, so.sha...]
    unnamed x120 -> x91, local copies, waits for them, and re-layouts: 5.13 us -> 42.7 us
    psum x1 -> x2, blocking collectives: 40.6 us -> 76.8 us  [the longest x1 39.1 us: local_step(): sq = lax.psum(jnp.where(sink, part, 0.0), 'data')]
    convert_element_type x2 -> x0, other arithmetic: 27.5 us -> none  [the longest x1 16.2 us: local_step(): (w_in[layer_idx] + perturb_coef * grad_in[layer_idx]).astype(jnp.bfloat16)]
    dot_general x88 -> x44, matrix products: 373 us -> 353 us  [dot(): return lax.dot_general(a, b, (dims, ((), ())), preferred_element_type=F32)]
    another operation x4 -> x7, other arithmetic: 55.7 us -> 45.7 us  [the longest x2 16.8 us: one_pass(): jnp.stack(s_in)]
  transfers between devices with their start and end apart: 2 -> 0, of which waited for: 2 -> 0; matrix products, arithmetic and copies ran while one was open for 0% -> 0% of each run, Pallas kernels for 0% -> 0%
where the time goes in v1:
time: 1010 us; the launch traced here: 998 us
  Pallas kernels  467 us (46%)
  matrix products  353 us (35%)
  blocking collectives  76.8 us (8%)
  other arithmetic  48.1 us (5%)
  local copies, waits for them, and re-layouts  47.9 us (5%)
    dot_general x44, matrix products, dot(): return lax.dot_general(a, b, (dims, ((), ())), preferred_element_type=F32)  353 us
    pallas_call x2, Pallas kernels, rs_only(): pl.pallas_call(functools.partial(rs_only_kernel, n, ns, nsl, lags, so.sha...  264 us
    pallas_call x2, Pallas kernels, ag_call(): pl.pallas_call(functools.partial(ag_kernel, n, ns, lags, order), out_shap...  203 us
    unnamed x91, local copies, waits for them, and re-layouts  42.7 us
    psum x1, blocking collectives, local_step(): sq = lax.psum(jnp.where(sink, part, 0.0), 'data')  39.1 us
    psum x1, blocking collectives, local_step(): loss = 0.5 * (lax.psum(sq2, 'data') * tok)  37.6 us

profile of v1, /device:TPU:0, one launch (start us, length us, event | category | flops | bytes accessed | tf_op | source)
XLA Modules:
  0.0 998.2 jit_solution(11422581619432918621)
XLA Ops:
  14.3 9.6 convert.14
  69.7 11.9 %convolution_bitcast_fusion.10 = f32[1,2048,512]{2,1,0:T(8,128)} fusion(bf16[1568,512]{1,0:T(8,128)(2,1)S(1)} %subtract_convert_fusion, bf16[1568,2048]{1,0:T(8,128)(2,1)} %convolution_convert_fusion.4), kind=kOutput, calls=%fused_computation.145 | convolution fusion | flops 3320446976 | bytes 12222464 | tf_op jit(solution)/shard_map/dot_general | solution.py:492
  81.5 13.1 %fusion.25 = bf16[1568,2048]{1,0:T(8,128)(2,1)S(1)} fusion(bf16[1568,2048]{1,0:T(8,128)(2,1)} %convolution_convert_fusion.4, bf16[1568,512]{1,0:T(8,128)(2,1)S(1)} %subtract_convert_fusion, bf16[4,2048,512]{2,1,0:T(8,128)(2,1)S(1)} %convert.15), kind=kOutput, calls=%fused_computation.66 | convolution fusion | flops 3355770880 | bytes 16547840 | tf_op jit(solution)/shard_map/dot_general | solution.py:492
  103.9 11.7 %convolution_bitcast_fusion.11 = f32[1,2048,512]{2,1,0:T(8,128)} fusion(bf16[1568,512]{1,0:T(8,128)(2,1)S(1)} %add_convert_fusion.8, bf16[1568,2048]{1,0:T(8,128)(2,1)} %copy-done.35), kind=kOutput, calls=%fused_computation.146 | convolution fusion | flops 3320446976 | bytes 12222464 | tf_op jit(solution)/shard_map/dot_general | solution.py:492
  115.6 13.1 %fusion.28 = bf16[1568,2048]{1,0:T(8,128)(2,1)S(1)} fusion(bf16[1568,2048]{1,0:T(8,128)(2,1)} %copy-done.35, bf16[1568,512]{1,0:T(8,128)(2,1)S(1)} %add_convert_fusion.8, bf16[4,2048,512]{2,1,0:T(8,128)(2,1)S(1)} %convert.15), kind=kOutput, calls=%fused_computation.69 | convolution fusion | flops 3355770880 | bytes 16547840 | tf_op jit(solution)/shard_map/dot_general | solution.py:492
  138.3 11.8 %convolution_bitcast_fusion.12 = f32[1,2048,512]{2,1,0:T(8,128)} fusion(bf16[1568,512]{1,0:T(8,128)(2,1)S(1)} %add_convert_fusion.7, bf16[1568,2048]{1,0:T(8,128)(2,1)} %convolution_convert_fusion.6), kind=kOutput, calls=%fused_computation.147 | convolution fusion | flops 3320446976 | bytes 12222464 | tf_op jit(solution)/shard_map/dot_general | solution.py:492
  150.2 12.9 %fusion.31 = bf16[1568,2048]{1,0:T(8,128)(2,1)S(1)} fusion(bf16[1568,2048]{1,0:T(8,128)(2,1)S(1)} %bitcast.182, bf16[1568,512]{1,0:T(8,128)(2,1)} %copy-done.37, bf16[4,2048,512]{2,1,0:T(8,128)(2,1)S(1)} %convert.15), kind=kOutput, calls=%fused_computation.72 | convolution fusion | flops 3355770880 | bytes 16547840 | tf_op jit(solution)/shard_map/dot_general | solution.py:492
  171.0 17.1 %fusion.83 = f32[1,512,2048]{2,1,0:T(8,128)} fusion(bf16[1568,512]{1,0:T(8,128)(2,1)S(1)} %copy-done.24, bf16[1568,2048]{1,0:T(8,128)(2,1)} %copy-done.34, bf16[1568,512]{1,0:T(8,128)(2,1)S(1)} %add_convert_fusion.6, bf16[4,2048,512]{2,1,0:T(8,128)(2,1)} %copy-done.8), kind=kOutput, calls=%fused_computation.150 | convolution fusion | flops 6644105216 | bytes 15925248 | tf_op jit(solution)/shard_map/dot_general | solution.py:492
  217.9 131.9 %rs_only.2 = (f32[32,2,16,256]{3,2,1,0:T(8,128)}, f32[32,2,16,256]{3,2,1,0:T(8,128)}) custom-call(f32[4,2048,512]{2,1,0:T(8,128)} %pad_maximum_fusion.so_ref, f32[4,512,2048]{2,1,0:T(8,128)} %pad_maximum_fusion.1.si_ref), custom_call_target="tpu_custom_call" | custom-call | tf_op jit(solution)/shard_map/rs_only/pallas_call | solution.py:285
  353.5 39.1 %psum.14 = f32[]{:T(128)} all-reduce(f32[]{:T(128)S(6)} %select_n.10), channel_id=1, replica_groups=mesh['data'=32] {'data'}, use_global_device_ids=true, to_apply=%region_2.3 | all-reduce | flops 1 | bytes 8 | tf_op jit(solution)/shard_map/psum | solution.py:542
  395.9 77.9 %gather.2 = (bf16[4,2048,512]{2,1,0:T(8,128)(2,1)S(1)}, bf16[4,512,2048]{2,1,0:T(8,128)(2,1)}) custom-call(f32[2]{0:T(128)S(1)} %pad_maximum_fusion.4.sc_ref, f32[32,2,16,256]{3,2,1,0:T(8,128)S(1)} %copy-done, f32[32,2,16,256]{3,2,1,0:T(8,128)S(1)} %copy-done.1, f32[4,2048,512]{2,1,0:T(8,128)} %wo_ref.3, f32[4,512,2048]{2,1,0:T(8,128)} %wi_ref.3), custom_call_target="tpu_custom_call" | custom-call | tf_op jit(solution)/shard_map/gather/pallas_call | solution.py:471
  473.8 8.7 convolution_convert_fusion
  519.5 8.6 multiply_reduce_fusion
  528.1 37.6 %psum.15 = f32[]{:T(128)} all-reduce(f32[]{:T(128)} %get-tuple-element.19), channel_id=1, replica_groups=mesh['data'=32] {'data'}, use_global_device_ids=true, to_apply=%region_4.5 | all-reduce | flops 1 | bytes 8 | tf_op jit(solution)/shard_map/psum | solution.py:551
  566.5 12.4 %convolution_bitcast_fusion.3 = f32[1,2048,512]{2,1,0:T(8,128)} fusion(bf16[1568,512]{1,0:T(8,128)(2,1)} %get-tuple-element.20, bf16[1568,2048]{1,0:T(8,128)(2,1)} %convolution_convert_fusion.1), kind=kOutput, calls=%fused_computation.138 | convolution fusion | flops 3320446976 | bytes 12222464 | tf_op jit(solution)/shard_map/dot_general | solution.py:492
  578.9 13.3 %fusion.16 = bf16[1568,2048]{1,0:T(8,128)(2,1)S(1)} fusion(bf16[1568,2048]{1,0:T(8,128)(2,1)} %convolution_convert_fusion.1, bf16[4,2048,512]{2,1,0:T(8,128)(2,1)S(1)} %copy-done.6, bf16[1568,512]{1,0:T(8,128)(2,1)S(1)} %copy-done.36), kind=kOutput, calls=%fused_computation.57 | convolution fusion | flops 3355770880 | bytes 16547840 | tf_op jit(solution)/shard_map/dot_general | solution.py:492
  601.6 11.7 %convolution_bitcast_fusion.4 = f32[1,2048,512]{2,1,0:T(8,128)} fusion(bf16[1568,512]{1,0:T(8,128)(2,1)S(1)} %add_convert_fusion.2, bf16[1568,2048]{1,0:T(8,128)(2,1)} %convolution_convert_fusion.2), kind=kOutput, calls=%fused_computation.139 | convolution fusion | flops 3320446976 | bytes 12222464 | tf_op jit(solution)/shard_map/dot_general | solution.py:492
  613.3 13.3 %fusion.19 = bf16[1568,2048]{1,0:T(8,128)(2,1)S(1)} fusion(bf16[1568,2048]{1,0:T(8,128)(2,1)} %convolution_convert_fusion.2, bf16[1568,512]{1,0:T(8,128)(2,1)S(1)} %add_convert_fusion.2, bf16[4,2048,512]{2,1,0:T(8,128)(2,1)S(1)} %copy-done.6), kind=kOutput, calls=%fused_computation.60 | convolution fusion | flops 3355770880 | bytes 16547840 | tf_op jit(solution)/shard_map/dot_general | solution.py:492
  636.0 11.9 %convolution_bitcast_fusion.5 = f32[1,2048,512]{2,1,0:T(8,128)} fusion(bf16[1568,512]{1,0:T(8,128)(2,1)S(1)} %add_convert_fusion.1, bf16[1568,2048]{1,0:T(8,128)(2,1)} %convolution_convert_fusion.3), kind=kOutput, calls=%fused_computation.140 | convolution fusion | flops 3320446976 | bytes 12222464 | tf_op jit(solution)/shard_map/dot_general | solution.py:492
  647.9 12.9 %fusion.22 = bf16[1568,2048]{1,0:T(8,128)(2,1)S(1)} fusion(bf16[1568,2048]{1,0:T(8,128)(2,1)} %convolution_convert_fusion.3, bf16[1568,512]{1,0:T(8,128)(2,1)S(1)} %add_convert_fusion.1, bf16[4,2048,512]{2,1,0:T(8,128)(2,1)S(1)} %copy-done.6), kind=kOutput, calls=%fused_computation.63 | convolution fusion | flops 3355770880 | bytes 16547840 | tf_op jit(solution)/shard_map/dot_general | solution.py:492
  667.2 17.2 %fusion.82 = f32[1,512,2048]{2,1,0:T(8,128)} fusion(bf16[1568,512]{1,0:T(8,128)(2,1)S(1)} %copy-done.25, bf16[2048,1568]{0,1:T(8,128)(2,1)} %convolution_convert_fusion, bf16[1568,512]{1,0:T(8,128)(2,1)S(1)} %add_convert_fusion, bf16[4,2048,512]{2,1,0:T(8,128)(2,1)} %copy-done.5), kind=kOutput, calls=%fused_computation.149 | convolution fusion | flops 6644105216 | bytes 15925248 | tf_op jit(solution)/shard_map/dot_general | solution.py:492
  714.5 132.4 %rs_only.3 = (f32[32,2,16,256]{3,2,1,0:T(8,128)}, f32[32,2,16,256]{3,2,1,0:T(8,128)}) custom-call(f32[4,2048,512]{2,1,0:T(8,128)} %pad_maximum_fusion.2.so_ref, f32[4,512,2048]{2,1,0:T(8,128)} %pad_maximum_fusion.3.si_ref), custom_call_target="tpu_custom_call" | custom-call | tf_op jit(solution)/shard_map/rs_only/pallas_call | solution.py:285
  849.3 124.7 %gather.3 = (f32[4,2048,512]{2,1,0:T(8,128)}, f32[4,512,2048]{2,1,0:T(8,128)}) custom-call(f32[2]{0:T(128)S(1)} %copy-done.4, f32[32,2,16,256]{3,2,1,0:T(8,128)S(1)} %copy-done.2, f32[32,2,16,256]{3,2,1,0:T(8,128)S(1)} %copy-done.3, f32[4,2048,512]{2,1,0:T(8,128)} %wo_ref.3, f32[4,512,2048]{2,1,0:T(8,128)} %wi_ref.3), custom_call_target="tpu_custom_call" | custom-call | tf_op jit(solution)/shard_map/gather/pallas_call | solution.py:471
  974.0 12.7 %copy.20 = f32[4,512,2048]{2,1,0:T(8,128)} copy(f32[4,512,2048]{2,1,0:T(8,128)} %get-tuple-element.28) | data formatting | bytes 33554432
  (131 shorter events, 225.1 us)
Async XLA Ops:
  14.2 135.9 %copy-start.8 = (bf16[4,2048,512]{2,1,0:T(8,128)(2,1)}, bf16[4,2048,512]{2,1,0:T(8,128)(2,1)S(1)}, u32[]{:S(2)}) copy-start(bf16[4,2048,512]{2,1,0:T(8,128)(2,1)S(1)} %convert.15) | copy-start | bytes 25165828
  14.2 9.6 copy-start.23
  132.4 5.9 copy-start.37
  132.4 17.7 %slice-start.4 = ((s8[6422528]{0:T(1024)(128)(4,1)}), s8[2228224]{0:T(1024)(128)(4,1)S(1)}, s32[]{:S(2)}) async-start(s8[6422528]{0:T(1024)(128)(4,1)} %bitcast.181), calls=%async_computation.4 | async-start | bytes 4456448
  138.3 11.8 %slice-start.5 = ((s8[6422528]{0:T(1024)(128)(4,1)}), s8[4194304]{0:T(1024)(128)(4,1)S(1)}, s32[]{:S(2)}) async-start(s8[6422528]{0:T(1024)(128)(4,1)} %bitcast.181), calls=%async_computation.5 | async-start | bytes 8388608
  188.1 8.3 copy-start.29
  188.1 8.4 copy-start.33
  201.1 8.4 copy-start.10
  201.1 8.6 copy-start.12
  201.1 10.4 %copy-start.16 = (f32[1,2048,512]{2,1,0:T(8,128)S(1)}, f32[1,2048,512]{2,1,0:T(8,128)}, u32[]{:S(2)}) copy-start(f32[1,2048,512]{2,1,0:T(8,128)} %convolution_bitcast_fusion.12) | copy-start | bytes 12582916
  473.8 45.7 %copy-start.5 = (bf16[4,2048,512]{2,1,0:T(8,128)(2,1)}, bf16[4,2048,512]{2,1,0:T(8,128)(2,1)S(1)}, u32[]{:S(2)}) copy-start(bf16[4,2048,512]{2,1,0:T(8,128)(2,1)S(1)} %get-tuple-element.14) | copy-start | bytes 25165828
  473.8 15.6 %slice-start = ((s8[8388608]{0:T(1024)(128)(4,1)}), s8[4194304]{0:T(1024)(128)(4,1)S(1)}, s32[]{:S(2)}) async-start(s8[8388608]{0:T(1024)(128)(4,1)} %bitcast.177), calls=%async_computation | async-start | bytes 8388608
  482.5 6.9 slice-start.1
  566.4 12.5 %copy-start.6 = (bf16[4,2048,512]{2,1,0:T(8,128)(2,1)S(1)}, bf16[4,2048,512]{2,1,0:T(8,128)(2,1)}, u32[]{:S(2)}) copy-start(bf16[4,2048,512]{2,1,0:T(8,128)(2,1)} %copy-done.5) | copy-start | bytes 25165828
  566.4 12.4 %copy-start.36 = (bf16[1568,512]{1,0:T(8,128)(2,1)S(1)}, bf16[1568,512]{1,0:T(8,128)(2,1)}, u32[]{:S(2)}) copy-start(bf16[1568,512]{1,0:T(8,128)(2,1)} %get-tuple-element.20) | copy-start | bytes 4816900
  566.5 25.7 %slice-start.2 = ((s8[8388608]{0:T(1024)(128)(4,1)}), s8[4194304]{0:T(1024)(128)(4,1)S(1)}, s32[]{:S(2)}) async-start(s8[8388608]{0:T(1024)(128)(4,1)} %bitcast.179), calls=%async_computation.2 | async-start | bytes 8388608
  578.9 13.3 %slice-start.3 = ((s8[8388608]{0:T(1024)(128)(4,1)}), s8[4194304]{0:T(1024)(128)(4,1)S(1)}, s32[]{:S(2)}) async-start(s8[8388608]{0:T(1024)(128)(4,1)} %bitcast.179), calls=%async_computation.3 | async-start | bytes 8388608
  684.5 8.6 copy-start.27
  684.5 8.6 copy-start.31
  697.7 8.4 copy-start.9
  697.7 8.6 copy-start.11
  697.7 10.4 %copy-start.15 = (f32[1,2048,512]{2,1,0:T(8,128)S(1)}, f32[1,2048,512]{2,1,0:T(8,128)}, u32[]{:S(2)}) copy-start(f32[1,2048,512]{2,1,0:T(8,128)} %convolution_bitcast_fusion.5) | copy-start | bytes 12582916
  714.5 132.4 %copy-start.4 = (f32[2]{0:T(128)S(1)}, f32[2]{0:T(128)}, u32[]{:S(2)}) copy-start(f32[2]{0:T(128)} %constant.55.clone.sc_ref) | copy-start | bytes 28
  974.0 16.4 %copy-start.7 = (f32[4,2048,512]{2,1,0:T(8,128)S(1)}, f32[4,2048,512]{2,1,0:T(8,128)}, u32[]{:S(2)}) copy-start(f32[4,2048,512]{2,1,0:T(8,128)} %get-tuple-element.29) | copy-start | bytes 50331652
  (20 other events, 74.4 us)

commit v2 on v0

v2 whole, which is shorter than its diff:
```python
import functools
import math

import jax
import jax.numpy as jnp
from jax import lax
from jax.experimental import pallas as pl
from jax.experimental.pallas import tpu as pltpu
from jax.sharding import PartitionSpec as P

MESH = pl.DeviceIdType.MESH
F32, BF = jnp.float32, jnp.bfloat16
RHO_FRAC = 0.1
LEARN_RATE = 1.0
D = 512
BLK = 256
PC = 16
RT = 784
BT = 1568
UNITS = 4
SUB, LANE = 8, 128
NZ = 4
HALF = 0.5
MIB = 2**20
GELU_A = math.sqrt(2.0 / math.pi)
GELU_B = 0.044715
TWO = AB = TYPES = DIRS = (0, 1)
SHAPES = ((BLK, D), (D, BLK))
ANY = pl.BlockSpec(memory_space=pl.ANY)
HBM = pl.BlockSpec(memory_space=pltpu.HBM)
VM = pl.BlockSpec(memory_space=pltpu.VMEM)
DMA = pltpu.SemaphoreType.DMA
rem = lax.rem
when = pl.when


def both(*conds):
    return functools.reduce(jnp.logical_and, conds)


def ds(start, size):
    return pl.ds(pl.multiple_of(start, SUB), size)


def cols(f):
    return pl.ds(pl.multiple_of(f * BLK, BLK), BLK)


def dg(a, b, ca, cb):
    return lax.dot_general(a, b, (((ca,), (cb,)), ((), ())), preferred_element_type=F32)


def scratch(dtype, *shape):
    return pltpu.VMEM(shape, dtype)


def local(src, dst, sem):
    return pltpu.make_async_copy(src, dst, sem)


def start(copies):
    for c in copies:
        c.start()


def wait(copies):
    for c in copies:
        c.wait()


class Geo:
    def __init__(self):
        me = lax.axis_index("data")
        flip = lambda step: me + step - 2 * step * rem(me // step, 2)
        self.me = me
        self.c, self.x, self.y, self.z = [rem(me // step, n) for step, n in ((1, 2), (2, 2), (4, 2), (8, NZ))]
        self.partner, self.xn, self.yn, self.z1, self.z2 = [flip(1 << k) for k in range(5)]
        self.zm, self.zp = me - 8, me + 8
        self.e = self.z // (NZ - 1)
        self.sink = rem(self.z, NZ - 1) == 0
        self.far = me + 24 - 48 * self.e
        self.w = (self.x, self.y)
        self.w2 = (self.y, self.x)
        self.n1 = (self.xn, self.yn)
        self.n2 = (self.yn, self.xn)

    def place(self, dirn):
        return self.z if dirn else NZ - 1 - self.z

    def enter(self, far=False, z2=False):
        bar = pltpu.get_barrier_semaphore()
        greet = lambda dev: pl.semaphore_signal(bar, device_id=(dev,), device_id_type=MESH)
        peers = [self.partner, self.xn, self.yn] + ([self.z2] if z2 else [])
        for dev in peers:
            greet(dev)
        when(self.z > 0)(lambda: greet(self.zm))
        when(self.z < NZ - 1)(lambda: greet(self.zp))
        if far:
            when(self.sink)(lambda: greet(self.far))
        n = len(peers) + 1
        when(self.sink)(lambda: pl.semaphore_wait(bar, n + int(far)))
        when(jnp.logical_not(self.sink))(lambda: pl.semaphore_wait(bar, n + 1))

    def half(self, T, c):
        R = SHAPES[T][0]
        return ds(c * (R // 2), R // 2)

    def part(self, T, ab, w):
        R = SHAPES[T][0]
        return self.c * (R // 2) + ab * (R // 4) + w * (R // 8)

    def zrow(self, T, ab, e):
        return self.part(T, ab, self.w[ab]) + e * (SHAPES[T][0] // 16)

    def fin(self, T, ab, mine):
        row = self.zrow(T, ab, self.e)
        w = self.w2[ab] if mine else 1 - self.w2[ab]
        if T:
            return ds(row + w * PC, PC), slice(None)
        return ds(row, PC), cols(w)


def region(out, T, li, f, rows, col=None):
    if T:
        return out[T].at[li, rows, cols(f)]
    return out[T].at[li, ds(f * BLK + rows.start, rows.size), slice(None) if col is None else col]


def schedule(s, j, lag, T):
    d = j - T - lag
    return None if d % 2 else s + d // 2


def run(k, n, what, T, *more):
    if k is not None:
        when(both(k >= 0, k < n))(functools.partial(what, T, k, *more))


class Scatter:
    FLOWS = FD, F1, F3, FM, FP = range(0, 10, 2)
    CREDITS = CD, C1, C3, CM, CP = range(0, 10, 2)

    def __init__(self, g, n, ns, nsl, lags, bufs, deliver):
        self.g, self.n, self.ns, self.nsl, self.deliver = g, n, ns, nsl, deliver
        self.S, self.rD, self.r1, self.rz, self.r3 = [bufs[2 * i : 2 * i + 2] for i in range(5)]
        self.ssem, self.rsem, self.cred = bufs[10:]
        ld, l1, self.lz, l3 = lags
        self.lam1 = ld
        self.lam2 = ld + l1
        self.lam4 = self.lam2 + (NZ - 1) * self.lz + l3

    @staticmethod
    def scratch(ns, nsl):
        out = []
        for lead, div, div2 in (((nsl,), 1, 1), ((ns,), 2, 1), ((ns, 2), 8, 1), ((ns, 2, 2), 16, 1), ((ns, 2), 0, 0)):
            for R, C in SHAPES:
                out.append(scratch(F32, *lead, *((R // div, C) if div else (PC, BLK))))
        return out + [DMA((2, 10, ns))] * 2 + [pltpu.SemaphoreType.REGULAR((2, 10))]

    def copy(self, T, flow, k, src, dst, dev):
        i = (T, flow, rem(k, self.ns))
        return pltpu.make_async_remote_copy(src, dst, self.ssem.at[i], self.rsem.at[i], device_id=(dev,), device_id_type=MESH)

    def take(self, T, credit, k):
        when(k >= self.ns)(lambda: pl.semaphore_wait(self.cred.at[T, credit]))

    def give(self, T, credit, k, dev):
        when(k + self.ns < self.n)(lambda: pl.semaphore_signal(self.cred.at[T, credit], device_id=(dev,), device_id_type=MESH))

    def slots(self, k):
        return rem(k, self.nsl), rem(k, self.ns)

    def to_core(self, T, k):
        s, q = self.slots(k)
        return self.copy(T, self.FD, k, self.S[T].at[s, self.g.half(T, 1 - self.g.c)], self.rD[T].at[q], self.g.partner)

    def first(self, T, k, ab):
        s, q = self.slots(k)
        rows = ds(self.g.part(T, ab, 1 - self.g.w[ab]), SHAPES[T][0] // 8)
        return self.copy(T, self.F1 + ab, k, self.S[T].at[s, rows], self.r1[T].at[q, ab], self.g.n1[ab])

    def zrows(self, T, ab, e):
        return ds(self.g.zrow(T, ab, e), SHAPES[T][0] // 16)

    def along(self, T, k, dirn, ab):
        s, q = self.slots(k)
        flow = (self.FP if dirn else self.FM) + ab
        src = self.S[T].at[s, self.zrows(T, ab, dirn)]
        return self.copy(T, flow, k, src, self.rz[T].at[q, ab, dirn], self.g.zp if dirn else self.g.zm)

    def last(self, T, k, ab):
        s, q = self.slots(k)
        return self.copy(T, self.F3 + ab, k, self.S[T].at[(s, *self.g.fin(T, ab, False))], self.r3[T].at[q, ab], self.g.n2[ab])

    def add(self, T, k, rows, val):
        s, _ = self.slots(k)
        self.S[T][s, rows] = self.S[T][s, rows] + val

    def begin(self, T, k):
        self.take(T, self.CD, k)
        self.to_core(T, k).start()

    def after_core(self, T, k):
        g = self.g
        self.to_core(T, k).wait()
        self.add(T, k, g.half(T, g.c), self.rD[T][rem(k, self.ns)])
        self.give(T, self.CD, k, g.partner)
        for ab in AB:
            self.take(T, self.C1 + ab, k)
            self.first(T, k, ab).start()

    def after_first(self, T, k):
        g = self.g
        for ab in AB:
            self.first(T, k, ab).wait()
        for ab in AB:
            self.add(T, k, ds(g.part(T, ab, g.w[ab]), SHAPES[T][0] // 8), self.r1[T][rem(k, self.ns), ab])
            self.give(T, self.C1 + ab, k, g.n1[ab])

    def line(self, T, k, dirn):
        g = self.g
        p = g.place(dirn)
        credit = self.CP if dirn else self.CM

        @when(k < self.n)
        def _():
            @when(p > 0)
            def _():
                for ab in AB:
                    self.along(T, k, dirn, ab).wait_recv()
                for ab in AB:
                    self.add(T, k, self.zrows(T, ab, dirn), self.rz[T][rem(k, self.ns), ab, dirn])
                self.give(T, credit, k, g.zm if dirn else g.zp)

            @when(p < NZ - 1)
            def _():
                self.take(T, credit, k)
                for ab in AB:
                    self.along(T, k, dirn, ab).start()

            @when(p == NZ - 1)
            def _():
                for ab in AB:
                    self.take(T, self.C3 + ab, k)
                    self.last(T, k, ab).start()

        @when(both(k > 0, p < NZ - 1))
        def _():
            for ab in AB:
                self.along(T, k - 1, dirn, ab).wait_send()

    def after_last(self, T, k):
        g = self.g

        @when(g.sink)
        def _():
            s, q = self.slots(k)
            for ab in AB:
                self.last(T, k, ab).wait()
            for ab in AB:
                self.deliver(T, k, ab, self.S[T][(s, *g.fin(T, ab, True))] + self.r3[T][q, ab])
                self.give(T, self.C3 + ab, k, g.n2[ab])

    def due(self, s, j):
        for T in TYPES:
            run(schedule(s, j, self.lam4, T), self.n, self.after_last, T)
        for T in TYPES:
            k = schedule(s, j, self.lam2, T)
            run(k, self.n, self.after_first, T)
            if k is not None:
                for dirn in DIRS:
                    run(k - self.g.place(dirn) * (self.lz // 2), self.n + 1, self.line, T, dirn)
        for T in TYPES:
            run(schedule(s, j, self.lam1, T), self.n, self.after_core, T)

    def steps(self):
        return self.n + (self.lam4 + 1) // 2 + 1


class Gather:
    FLOWS = F3, FM, FP, FE0, FE1, FD = range(6)

    def __init__(self, g, n, nf, layer, lags, own, out, sems, start=0):
        self.g, self.n, self.nf, self.layer, self.own, self.out = g, n, nf, layer, own, out
        self.ssem, self.rsem, self.lsem = sems
        self.ns = self.ssem.shape[-1]
        l3, self.lz, le, ld = lags
        self.mu0 = start
        self.mu1 = start + l3
        self.mu2 = self.mu1 + (NZ - 1) * self.lz + le
        self.mu3 = self.mu2 + ld

    @staticmethod
    def scratch(n, ns):
        return [DMA((2, 6, ns)), DMA((2, 6, n)), DMA((2, 2, ns))]

    def region(self, T, k, rows, col=None):
        return region(self.out, T, self.layer(k // self.nf), rem(k, self.nf), rows, col)

    def rows(self, T, k, row, div):
        return self.region(T, k, ds(row, SHAPES[T][0] // div))

    def copy(self, T, flow, k, src, dst, dev):
        return pltpu.make_async_remote_copy(src, dst, self.ssem.at[T, flow, rem(k, self.ns)], self.rsem.at[T, flow, k],
            device_id=(dev,), device_id_type=MESH)

    def keep(self, T, k, ab):
        rows, col = self.g.fin(T, ab, True)
        return local(self.own[T].at[k, ab], self.region(T, k, rows, col), self.lsem.at[T, ab, rem(k, self.ns)])

    def begin(self, T, k):
        g = self.g

        @when(g.sink)
        def _():
            for ab in AB:
                rows, col = g.fin(T, ab, True)
                self.keep(T, k, ab).start()
                self.copy(T, self.F3, k, self.own[T].at[k, ab], self.region(T, k, rows, col), g.n2[ab]).start()

    def over(self, T, flow, k, ref, send=True, recv=True):
        if send:
            local(ref, ref, self.ssem.at[T, flow, rem(k, self.ns)]).wait()
        if recv:
            local(ref, ref, self.rsem.at[T, flow, k]).wait()

    def line(self, T, k, dirn):
        g = self.g
        p = g.place(dirn)
        e = 1 - dirn
        flow = self.FP if dirn else self.FM
        pair = lambda k: self.rows(T, k, 0, 8)

        @when(k < self.n)
        def _():
            @when(p == 0)
            def _():
                for ab in AB:
                    self.keep(T, k, ab).wait()
                self.over(T, self.F3, k, self.own[T].at[k])

            when(p > 0)(lambda: self.over(T, flow, k, pair(k), send=False))
            parts = [self.rows(T, k, g.zrow(T, ab, e), 16) for ab in AB]

            @when(p < NZ - 1)
            def _():
                for r in parts:
                    self.copy(T, flow, k, r, r, g.zp if dirn else g.zm).start()

            for ab in AB:
                self.copy(T, self.FE0 + e, k, parts[ab], parts[ab], g.n1[ab]).start()

        when(both(k > 0, p < NZ - 1))(lambda: self.over(T, flow, k - 1, pair(k - 1), recv=False))

    def to_core(self, T, k):
        r = self.region(T, k, self.g.half(T, self.g.c))
        return self.copy(T, self.FD, k, r, r, self.g.partner)

    def after_first(self, T, k):
        for e in TWO:
            self.over(T, self.FE0 + e, k, self.rows(T, k, 0, 8))
        self.to_core(T, k).start()

    def done(self, T, k):
        self.to_core(T, k).wait()

    def due(self, s, j):
        for T in TYPES:
            run(schedule(s, j, self.mu0, T), self.n, self.begin, T)
        for T in TYPES:
            k = schedule(s, j, self.mu1, T)
            if k is not None:
                for dirn in DIRS:
                    run(k - self.g.place(dirn) * (self.lz // 2), self.n + 1, self.line, T, dirn)
        for T in TYPES:
            run(schedule(s, j, self.mu2, T), self.n, self.after_first, T)
            run(schedule(s, j, self.mu3, T), self.n, self.done, T)

    def steps(self):
        return self.n + (self.mu3 + 1) // 2 + 1


class PairSum:
    GAP = 3

    def __init__(self, devs, bufs):
        self.devs = devs
        self.part, self.nbr, self.ssem, self.rsem = bufs

    @staticmethod
    def scratch(n):
        return [scratch(F32, n + 1, SUB, LANE), scratch(F32, n, SUB, LANE), DMA((n,)), DMA((n,))]

    def copy(self, r):
        return pltpu.make_async_remote_copy(self.part.at[r], self.nbr.at[r], self.ssem.at[r], self.rsem.at[r],
            device_id=(self.devs[r],), device_id_type=MESH)

    def finish(self, r):
        self.copy(r).wait()
        self.part[r + 1] = self.part[r] + self.nbr[r]

    def due(self, s):
        for r in range(len(self.devs)):
            when(s == r * self.GAP)(lambda: self.copy(r).start())
            when(s == r * self.GAP + self.GAP - 1)(lambda: self.finish(r))

    def now(self):
        for r in range(len(self.devs)):
            self.copy(r).start()
            self.finish(r)


def gelu(z):
    half = HALF * z
    return half + half * jnp.tanh(z * (GELU_A + (GELU_A * GELU_B) * (z * z)))


def gelu_parts(z):
    zz = z * z
    t = jnp.tanh(z * (GELU_A + (GELU_A * GELU_B) * zz))
    half = HALF * z
    slope = (HALF + HALF * t) + half * ((1 - t * t) * (GELU_A + (3 * GELU_A * GELU_B) * zz))
    return half + half * t, slope


class Forward:
    def __init__(self, nl, tok, hbm, outs, bufs):
        self.nl, self.nt = nl, tok // RT
        self.x, self.y = hbm
        self.h_o, self.z_o, self.q_o, self.loss = outs
        self.h, self.yb, self.a, self.zt, self.wi, self.wo, self.hsem, self.zsem, self.ysem = bufs
        self.dff = self.a.shape[1]

    @staticmethod
    def scratch(tok, dff):
        return [scratch(BF, tok, D), scratch(BF, tok, D), scratch(BF, RT, dff), scratch(BF, 2, RT, dff),
                scratch(BF, 2, D, dff), scratch(BF, 2, dff, D), DMA((tok // RT,)), DMA((2, 2)), DMA((2,))]

    def h_copy(self, r, dst):
        rows = ds(r * RT, RT)
        return local(self.h.at[rows], dst.at[rows], self.hsem.at[r])

    def prologue(self):
        self.cy = local(self.y, self.yb, self.ysem.at[1])
        cx = local(self.x, self.h, self.ysem.at[0])
        cx.start()
        self.cy.start()
        self.loss[...] = jnp.zeros_like(self.loss)
        cx.wait()
        for r in range(self.nt):
            self.h_copy(r, self.h_o.at[0]).start()

    def z_copy(self, li, r, i, slot):
        c = pl.ds(i * (self.dff // 2), self.dff // 2)
        return local(self.zt.at[slot, :, c], self.z_o.at[li, ds(r * RT, RT), c], self.zsem.at[slot, i])

    def z_unit(self, li, r, w, i):
        slot = rem(li * self.nt + r, 2)
        when(li * self.nt + r > 1)(lambda: self.z_copy(0, 0, i, slot).wait())
        h = self.h[ds(r * RT, RT)]
        per = self.dff // D // 2
        for b in range(i * per, i * per + per):
            c = pl.ds(b * D, D)
            z = dg(h, self.wi[w, :, c], 1, 0).astype(BF)
            self.zt[slot, :, c] = z
            self.a[:, c] = gelu(z.astype(F32)).astype(BF)
        self.z_copy(li, r, i, slot).start()

    def h_unit(self, li, r, w, i):
        rows, c = ds(r * RT, RT), pl.ds(i * BLK, BLK)
        hn = (self.h[rows, c].astype(F32) + dg(self.a[...], self.wo[w, :, c], 1, 0)).astype(BF)
        if i == 0:
            self.h_copy(r, self.h_o.at[0]).wait()

        @when(li < self.nl - 1)
        def _():
            self.h[rows, c] = hn
            if i:
                self.h_copy(r, self.h_o.at[li + 1]).start()

        @when(li == self.nl - 1)
        def _():
            if i == 0:
                when(r == 0)(self.cy.wait)
            err = hn.astype(F32) - self.yb[rows, c].astype(F32)
            self.h[rows, c] = err.astype(BF)
            if i:
                self.h_copy(r, self.q_o).start()
            sq = jnp.sum((err * err).reshape(RT // SUB, SUB, BLK), axis=0)
            for b in range(BLK // LANE):
                self.loss[...] += sq[:, b * LANE : (b + 1) * LANE]

    def unit(self, k):
        return functools.partial(self.h_unit if k // 2 else self.z_unit, i=k % 2)

    def epilogue(self):
        for slot in TWO:
            for i in TWO:
                self.z_copy(0, 0, i, slot).wait()
        for r in range(self.nt):
            self.h_copy(r, self.q_o).wait()

    @staticmethod
    def shapes(nl, tok, dff):
        S = jax.ShapeDtypeStruct
        return [S((nl, tok, D), BF), S((nl, tok, dff), BF), S((tok, D), BF), S((SUB, LANE), F32)]


def forward_kernel(nl, tok, x, y, w_out, w_in, h_o, z_o, q_o, loss, wi32, wo32, wsem, *bufs):
    fw = Forward(nl, tok, (x, y), (h_o, z_o, q_o, loss), bufs)
    shares = [(ds(r * (m.shape[1] // fw.nt), m.shape[1] // fw.nt), m, v, w) for m, v, w in ((w_in, wi32, fw.wi), (w_out, wo32, fw.wo)) for r in range(fw.nt)]

    def loads(li, r):
        return [local(m.at[li, rows], v.at[rows], wsem.at[r, i]) for i, (rows, m, v, _) in enumerate(shares[r :: fw.nt])]

    def take(li, r, last):
        if not last:
            wait(loads(li, r))
        for rows, _, v, w in shares[r :: fw.nt]:
            w[rem(li, 2), rows] = v[rows].astype(BF)
        when(li + 1 < nl)(lambda: start(loads(li + 1, r)))

    for r in range(fw.nt):
        start(loads(0, r))
    fw.prologue()
    for r in range(fw.nt):
        take(0, r, False)

    def body(li, _):
        for r in range(fw.nt):
            when(li + 1 < nl)(lambda: wait(loads(li + 1, r)))
            take(li + 1, r, True)
            for k in range(UNITS):
                fw.unit(k)(li, r, rem(li, 2))
        return 0

    lax.fori_loop(0, nl, body, 0)
    fw.epilogue()


def forward(x, y, w_out, w_in):
    nl, dff, _ = w_out.shape
    tok = x.shape[0]
    return pl.pallas_call(
        functools.partial(forward_kernel, nl, tok),
        out_shape=Forward.shapes(nl, tok, dff),
        in_specs=[HBM] * 4,
        out_specs=[HBM] * 3 + [VM],
        scratch_shapes=[scratch(F32, D, dff), scratch(F32, dff, D), DMA((tok // RT, 2))] + Forward.scratch(tok, dff),
        compiler_params=pltpu.CompilerParams(vmem_limit_bytes=56 * MIB),
        name="forward",
    )(x, y, w_out, w_in)


def gather_forward_kernel(nl, tok, lags, pe_o, pe_i, x, y, wo_o, wi_o, h_o, z_o, q_o, loss, own_o, own_i, wsem, *bufs):
    g = Geo()
    n = pe_o.shape[0]
    nf = n // nl
    ga = Gather(g, n, nf, lambda q: q, lags, (own_o, own_i), (wo_o, wi_o), bufs[:3])
    fw = Forward(nl, tok, (x, y), (h_o, z_o, q_o, loss), bufs[3:])
    pieces = [local(src, dst, wsem.at[i]) for i, (src, dst) in enumerate(((pe_o, own_o), (pe_i, own_i)))]
    start(pieces)
    loads = lambda li: [local(wi_o.at[li], fw.wi.at[rem(li, 2)], wsem.at[0]), local(wo_o.at[li], fw.wo.at[rem(li, 2)], wsem.at[1])]
    fw.prologue()
    g.enter()
    wait(pieces)
    lead = (ga.mu3 + 1) // 2 + nf

    def body(s, _):
        ga.due(s, 0)
        u = s - lead
        up = jnp.maximum(u, 0)
        li, i = up // nf, rem(up, nf)

        @when(both(u >= 0, i == 0))
        def _():
            wait(loads(li))

        for k in range(UNITS):
            when(both(u >= 0, i < fw.nt * UNITS, rem(i, UNITS) == k))(lambda: fw.unit(k)(li, i // UNITS, rem(li, 2)))
        ga.due(s, 1)

        @when(both(u + 1 >= 0, rem(u + 1 + n, nf) == 0, u + 1 < n))
        def _():
            start(loads((u + 1) // nf))

        return 0

    lax.fori_loop(0, lead + n, body, 0)
    fw.epilogue()


def gather_forward(pe_o, pe_i, x, y, nl, ns=4, lags=(4, 4, 4, 2), cid=2):
    n, tok = pe_o.shape[0], x.shape[0]
    dff = n // nl * BLK
    S = jax.ShapeDtypeStruct
    return pl.pallas_call(
        functools.partial(gather_forward_kernel, nl, tok, lags),
        out_shape=[S((nl, dff, D), BF), S((nl, D, dff), BF)] + Forward.shapes(nl, tok, dff),
        in_specs=[HBM] * 4,
        out_specs=[HBM] * 5 + [VM],
        scratch_shapes=[scratch(BF, n, 2, PC, BLK)] * 2 + [DMA((2,))] + Gather.scratch(n, ns) + Forward.scratch(tok, dff),
        cost_estimate=pl.CostEstimate(flops=tok * D * dff * nl * 4, bytes_accessed=60 * MIB, transcendentals=0),
        compiler_params=pltpu.CompilerParams(collective_id=cid, has_side_effects=True, vmem_limit_bytes=48 * MIB),
        name="gather_forward",
    )(pe_o, pe_i, x, y)


class Backward:
    def __init__(self, nl, tok, hbm, bufs):
        self.nl, self.tok = nl, tok
        self.q_h, self.h_h, self.z_h, self.wo_h, self.wi_h = hbm
        self.q, self.h, self.z, self.wo, self.wi, self.a, self.p, self.acc, self.sem = bufs
        self.nf = self.z_h.shape[-1] // BLK
        self.n = nl * self.nf

    @staticmethod
    def scratch(tok, wdt):
        return [scratch(BF, tok, D), scratch(BF, 2, tok, D), scratch(BF, 2, tok, BLK), scratch(wdt, 2, BLK, D), scratch(wdt, 2, D, BLK),
                scratch(BF, tok, BLK), scratch(BF, tok, BLK), scratch(F32, tok, D), DMA((5, 2))]

    def at(self, s):
        return self.nl - 1 - s // self.nf, rem(s, self.nf), rem(s, 2)

    def load_h(self, li):
        i = rem(li, 2)
        return local(self.h_h.at[li], self.h.at[i], self.sem.at[0, i])

    def loads(self, s):
        li, f, b = self.at(s)
        return [local(src, dst.at[b], self.sem.at[i + 1, b]) for i, (src, dst) in enumerate((
            (self.z_h.at[li, :, cols(f)], self.z), (self.wo_h.at[li, cols(f)], self.wo), (self.wi_h.at[li, :, cols(f)], self.wi)))]

    def prologue(self):
        cq = local(self.q_h, self.q, self.sem.at[4, 0])
        for c in [cq, *self.loads(0), self.load_h(self.nl - 1)]:
            c.start()
        cq.wait()
        self.acc[...] = self.q[...].astype(F32)

    def tiles(self):
        return [pl.ds(r * BT, BT) for r in range(self.tok // BT)]

    def out_block(self, s, dst):
        li, f, b = self.at(s)
        wait(self.loads(s))

        @when(s + 1 < self.n)
        def _():
            start(self.loads(s + 1))

        @when(f == 0)
        def _():
            self.load_h(li).wait()
            when(li > 0)(lambda: self.load_h(li - 1).start())

        wo = self.wo[b].astype(BF)
        for rows in self.tiles():
            a, slope = gelu_parts(self.z[b, rows].astype(F32))
            self.a[rows] = a.astype(BF)
            self.p[rows] = (dg(self.q[rows], wo, 1, 1) * slope).astype(BF)
        dst[...] = dg(self.a[...], self.q[...], 0, 0)

    def in_block(self, s, dst):
        li, f, b = self.at(s)
        dst[...] = dg(self.h[rem(li, 2)], self.p[...], 0, 0)

        @when(li > 0)
        def _():
            wi = self.wi[b].astype(BF)
            for rows in self.tiles():
                self.acc[rows] = self.acc[rows] + dg(self.p[rows], wi, 1, 1)

            @when(f == self.nf - 1)
            def _():
                for rows in self.tiles():
                    q = self.acc[rows].astype(BF)
                    self.q[rows] = q
                    self.acc[rows] = q.astype(F32)


def load_owned(g, n, nf, layer, mats, dst, sem):
    def issue(k, _):
        for T in TYPES:
            for ab in AB:
                rows, col = g.fin(T, ab, True)
                local(region(mats, T, layer(k // nf), rem(k, nf), rows, col), dst[T].at[k, ab], sem.at[T]).start()
        return 0

    lax.fori_loop(0, n, issue, 0)


def wait_owned(dst, sem):
    for T in TYPES:
        local(dst[T], dst[T], sem.at[T]).wait()


def backward_kernel(nl, tok, ns, nsl, lags, glags, norm, scale, coef, *refs):
    q_h, h_h, z_h, wo_h, wi_h, refs = *refs[:5], refs[5:]
    if norm:
        mats = wo_h, wi_h
    else:
        mats, tile, refs = refs[:2], refs[2], refs[3:]
    bw_hbm = q_h, h_h, z_h, wo_h, wi_h
    n = nl * (z_h.shape[-1] // BLK)
    nf = n // nl
    last_first = lambda q: nl - 1 - q
    out, refs = refs[:2], refs[2:]
    if not norm:
        loss, refs = refs[0], refs[1:]
    n_sc = len(Scatter.scratch(ns, nsl))
    sc_bufs, refs = refs[:n_sc], refs[n_sc:]
    bw, refs = Backward(nl, tok, bw_hbm, refs[:9]), refs[9:]
    w_p, wsem, refs = refs[:2], refs[2], refs[3:]
    g = Geo()
    bw.prologue()
    when(g.sink)(lambda: load_owned(g, n, nf, last_first, mats, w_p, wsem))
    if norm:
        own, pieces, sq, pair = refs[:2], refs[2:4], refs[4], refs[5:]
        ps = PairSum((g.partner, g.xn, g.yn, g.far), pair)
        sq[...] = jnp.zeros_like(sq)
    else:
        ps = PairSum((g.partner, g.xn, g.yn, g.z1, g.z2), refs[:4])
        ps.part[0] = tile[...]

    def deliver(T, k, ab, val):
        val = val * scale
        if norm:
            own[T][k, ab] = val
            sq[...] += val * val
        else:
            w_p[T][k, ab] = w_p[T][k, ab] - coef * val

    g.enter(far=norm, z2=not norm)
    sc = Scatter(g, n, ns, nsl, lags, sc_bufs, deliver)
    steps = sc.steps()
    if not norm:
        ga = Gather(g, n, nf, last_first, glags, w_p, out, refs[4:], sc.lam4 + 1)
        steps = ga.steps()

    def body(s, _):
        when(both(s == 1, g.sink))(lambda: wait_owned(w_p, wsem))
        for j, block in enumerate((bw.out_block, bw.in_block)):

            @when(s < n)
            def _():
                block(s, sc.S[j].at[rem(s, nsl)])
                sc.begin(j, s)

            sc.due(s, j)
            if not norm:
                ga.due(s, j)
        if not norm:
            ps.due(s)
        return 0

    lax.fori_loop(0, steps, body, 0)
    if not norm:
        loss[...] = ps.part[5]
        return

    @when(g.sink)
    def _():
        quarters = [sq[i * SUB : (i + 1) * SUB, j * LANE : (j + 1) * LANE] for i in TWO for j in TWO]
        ps.part[0] = sum(quarters[1:], quarters[0])
        ps.now()
        step = coef / jnp.sqrt(jnp.broadcast_to(jnp.sum(ps.part[4]), (1, 1)))

        def piece(k, _):
            to = (nl - 1 - k // nf) * nf + rem(k, nf)
            for T in TYPES:
                pieces[T][to] = (w_p[T][k] + step * own[T][k]).astype(BF)
            return 0

        lax.fori_loop(0, n, piece, 0)
        copies = [local(pieces[T], out[T], wsem.at[T]) for T in TYPES]
        start(copies)
        wait(copies)


def backward(q, h, z, wo, wi, scale, coef, new=None, ns=4, nsl=10, lags=(1, 4, 2, 4), glags=(4, 4, 4, 2), cid=1):
    nl, tok, dff = z.shape
    n = nl * dff // BLK
    norm = new is None
    S = jax.ShapeDtypeStruct
    piece = lambda dt: scratch(dt, n, 2, PC, BLK)
    scr = Scatter.scratch(ns, nsl) + Backward.scratch(tok, wo.dtype) + [piece(F32)] * 2 + [DMA((2,))]
    if norm:
        scr += [piece(F32)] * 2 + [piece(BF)] * 2 + [scratch(F32, PC, BLK)] + PairSum.scratch(4)
        outs, specs, more = [S((n, 2, PC, BLK), BF)] * 2, [HBM] * 2, ()
    else:
        scr += PairSum.scratch(5) + Gather.scratch(n, ns)
        outs, specs, more = [S(new[0].shape, F32), S(new[1].shape, F32), S((SUB, LANE), F32)], [HBM] * 2 + [VM], new
    return pl.pallas_call(
        functools.partial(backward_kernel, nl, tok, ns, nsl, lags, glags, norm, scale, coef),
        out_shape=outs,
        in_specs=[HBM] * 5 + [HBM, HBM, VM][: len(more)],
        out_specs=specs,
        scratch_shapes=scr,
        cost_estimate=pl.CostEstimate(flops=tok * D * dff * nl * 8, bytes_accessed=60 * MIB, transcendentals=0),
        compiler_params=pltpu.CompilerParams(collective_id=cid, has_side_effects=True, vmem_limit_bytes=56 * MIB),
        name="backward_norm" if norm else "backward_update",
    )(q, h, z, wo, wi, *more)


def solution(mesh):
    n_dev = mesh.shape["data"]

    def local_step(x_loc, y_loc, w_in, w_out):
        nl, d_model, d_ff = w_in.shape
        scale = 1.0 / (x_loc.shape[0] * n_dev * x_loc.shape[1] * d_model)
        rho = RHO_FRAC * math.sqrt(nl * (d_model + d_ff))
        x, y = [v.reshape(-1, d_model) for v in (x_loc, y_loc)]
        h, z, q, _ = forward(x, y, w_out, w_in)
        pieces = backward(q, h, z, w_out, w_in, scale, rho, cid=1)
        wo, wi, h, z, q, tile = gather_forward(*pieces, x, y, nl, cid=2)
        new_out, new_in, tile = backward(q, h, z, wo, wi, scale, LEARN_RATE, (w_out, w_in, tile), cid=3)
        return new_in, new_out, HALF * (jnp.sum(tile) * scale)

    specs = P("data"), P("data"), P(), P()
    return jax.shard_map(local_step, mesh=mesh, in_specs=specs, out_specs=(P(), P(), P()), check_vma=False)
```

time: 1520 us -> 604 us (0.40)
  waiting for transfers between devices: 957 us -> 0 us
  Pallas kernels: 0 us -> 567 us
  matrix products: 373 us -> 0 us
  other arithmetic: 101 us -> 1.29 us
  blocking collectives: 40.6 us -> 0 us
  between operations: 23.7 us -> 2.51 us
    psum x2 -> x0, waiting for transfers between devices: 957 us -> none  [the longest x1 501 us: local_step(): grad_out = [lax.psum(part_sum, 'data') * tok_scale for part_sum in sums_out]]
    pallas_call x0 -> x4, Pallas kernels: none -> 567 us  [the longest x2 404 us: backward(): pl.pallas_call(functools.partial(backward_kernel, nl, tok, ns, nsl, lags,...]
    dot_general x88 -> x0, matrix products: 373 us -> none  [the longest x16 100 us: micro_grads(): jnp.einsum('bsf,bsd->fd', gelu_out.astype(jnp.bfloat16), back_grad, prefe...]
    another operation x4 -> x0, other arithmetic: 55.7 us -> none  [the longest x2 27.9 us: local_step(): jnp.stack([w_in[layer_idx] - LEARN_RATE * (total_in[layer_idx] * tok_scal...]
    psum x1 -> x0, blocking collectives: 40.6 us -> none  [local_step(): total_sq = lax.psum(second_sq, 'data')]
    convert_element_type x2 -> x0, other arithmetic: 27.5 us -> none  [the longest x1 16.2 us: local_step(): (w_in[layer_idx] + perturb_coef * grad_in[layer_idx]).astype(jnp.bfloat16)]
    unnamed x120 -> x18, local copies, waits for them, and re-layouts: 5.13 us -> 30.2 us
    reduce_sum x4 -> x1, other arithmetic: 17.4 us -> 1.29 us  [local_step(): return (new_in, new_out, HALF * (jnp.sum(tile) * scale))]
  transfers between devices with their start and end apart: 2 -> 0, of which waited for: 2 -> 0; matrix products, arithmetic and copies ran while one was open for 0% -> 0% of each run, Pallas kernels for 0% -> 0%
where the time goes in v2:
time: 604 us; the launch traced here: 603 us
  Pallas kernels  567 us (94%)
  local copies, waits for them, and re-layouts  32.9 us (5%)
    pallas_call x2, Pallas kernels, backward(): pl.pallas_call(functools.partial(backward_kernel, nl, tok, ns, nsl, lags,...  404 us
    pallas_call x1, Pallas kernels, gather_forward(): pl.pallas_call(functools.partial(gather_forward_kernel, nl, tok, lags), o...  102 us
    pallas_call x1, Pallas kernels, forward(): pl.pallas_call(functools.partial(forward_kernel, nl, tok), out_shape=Forw...  60.9 us
    unnamed x18, local copies, waits for them, and re-layouts  30.2 us

profile of v2, /device:TPU:0, one launch (start us, length us, event | category | flops | bytes accessed | tf_op | source)
XLA Modules:
  0.0 603.5 jit_solution(9689244785124888860)
XLA Ops:
  0.6 1.9 copy.9
  2.6 1.3 reshape.12.x
  3.9 1.9 copy.10
  5.8 1.3 reshape.13.y
  7.1 60.9 %forward.1 = (bf16[4,1568,512]{2,1,0:T(8,128)(2,1)}, bf16[4,1568,2048]{2,1,0:T(8,128)(2,1)}, bf16[1568,512]{1,0:T(8,128)(2,1)}, f32[8,128]{1,0:T(8,128)}) custom-call(bf16[1568,512]{1,0:T(8,128)(2,1)} %reshape.12.x, bf16[1568,512]{1,0:T(8,128)(2,1)} %reshape.13.y, f32[4,2048,512]{2,1,0:T(8,128)} %refs_5_.1, f32[4,512,2048]{2,1,0:T(8,128)} %refs_6_.1), custom_call_target="tpu_custom_call" | custom-call | tf_op jit(solution)/shard_map/forward/pallas_call | solution.py:544
  68.0 0.0 copy-start
  68.0 0.0 copy-start.1
  68.0 159.8 %backward_norm.1 = (bf16[32,2,16,256]{3,2,1,0:T(8,128)(2,1)}, bf16[32,2,16,256]{3,2,1,0:T(8,128)(2,1)}) custom-call(bf16[1568,512]{1,0:T(8,128)(2,1)} %get-tuple-element.17.refs_0_, bf16[4,1568,512]{2,1,0:T(8,128)(2,1)} %get-tuple-element.18.refs_1_, bf16[4,1568,2048]{2,1,0:T(8,128)(2,1)} %get-tuple-element.19.refs_2_, f32[4,2048,512]{2,1,0:T(8,128)} %refs_5_.1, ...), custom_call_target="tpu_custom_call" | custom-call | flops 52613349376 | bytes 62914560 | tf_op jit(solution)/shard_map/backward_norm/pallas_call | solution.py:794
  227.8 0.0 copy-done
  227.8 0.0 copy-done.1
  227.8 0.0 copy-start.3
  227.8 1.0 copy-done.3
  228.9 0.0 copy-start.4
  228.9 1.0 copy-done.4
  229.9 102.1 %gather_forward.1 = (bf16[4,2048,512]{2,1,0:T(8,128)(2,1)}, bf16[4,512,2048]{2,1,0:T(8,128)(2,1)}, bf16[4,1568,512]{2,1,0:T(8,128)(2,1)}, bf16[4,1568,2048]{2,1,...) custom-call(bf16[32,2,16,256]{3,2,1,0:T(8,128)(2,1)S(1)} %copy-done.3, ...), custom_call_target="tpu_custom_call" | custom-call | flops 26306674688 | bytes 62914560 | tf_op jit(solution)/shard_map/gather_forward/pallas_call | solution.py:597
  332.0 0.0 copy-start.2
  332.0 1.1 copy-done.2
  333.1 0.6 copy-done.5
  333.7 244.1 %backward_update.1 = (f32[4,2048,512]{2,1,0:T(8,128)}, f32[4,512,2048]{2,1,0:T(8,128)}, f32[8,128]{1,0:T(8,128)}) custom-call(bf16[1568,512]{1,0:T(8,128)(2,1)} %copy-done.2, bf16[4,1568,512]{2,1,0:T(8,128)(2,1)} %get-tuple-element.23.refs_1_, bf16[4,1568,2048]{2,1,0:T(8,128)(2,1)} %get-tuple-element.24.refs_2_, ...), custom_call_target="tpu_custom_call" | custom-call | flops 52613349376 | bytes 62914560 | tf_op jit(solution)/shard_map/backward_update/pallas_call | solution.py:794
  577.8 1.3 reduce_sum.9
  579.8 0.0 copy-start.6
  579.8 12.7 %copy.13 = f32[4,512,2048]{2,1,0:T(8,128)} copy(f32[4,512,2048]{2,1,0:T(8,128)} %get-tuple-element.34) | data formatting | bytes 33554432
  592.5 3.7 copy-done.6
  596.2 6.2 %copy.14 = f32[4,2048,512]{2,1,0:T(8,128)} copy(f32[4,2048,512]{2,1,0:T(8,128)S(1)} %copy-done.6) | data formatting | bytes 33554432
  (1 shorter events, 0.0 us)
Async XLA Ops:
  68.0 159.8 %copy-start = (bf16[1568,512]{1,0:T(8,128)(2,1)S(1)}, bf16[1568,512]{1,0:T(8,128)(2,1)}, u32[]{:S(2)}) copy-start(bf16[1568,512]{1,0:T(8,128)(2,1)} %reshape.12.x) | copy-start | bytes 4816900
  68.0 159.8 %copy-start.1 = (bf16[1568,512]{1,0:T(8,128)(2,1)S(1)}, bf16[1568,512]{1,0:T(8,128)(2,1)}, u32[]{:S(2)}) copy-start(bf16[1568,512]{1,0:T(8,128)(2,1)} %reshape.13.y) | copy-start | bytes 4816900
  227.8 1.0 copy-start.3
  228.9 1.0 copy-start.4
  332.0 1.2 copy-start.2
  333.1 0.6 copy-start.5
  579.8 16.4 %copy-start.6 = (f32[4,2048,512]{2,1,0:T(8,128)S(1)}, f32[4,2048,512]{2,1,0:T(8,128)}, u32[]{:S(2)}) copy-start(f32[4,2048,512]{2,1,0:T(8,128)} %get-tuple-element.35) | copy-start | bytes 50331652

commit v3 on v2

--- a/solution.py
+++ b/solution.py
@@ -15,9 +15,8 @@
 D = 512
 BLK = 256
 PC = 16
-RT = 784
+FT = 224
 BT = 1568
-UNITS = 4
 SUB, LANE = 8, 128
 NZ = 4
 HALF = 0.5
@@ -424,117 +423,99 @@
 
 
 class Forward:
-    def __init__(self, nl, tok, hbm, outs, bufs):
-        self.nl, self.nt = nl, tok // RT
-        self.x, self.y = hbm
+    def __init__(self, nl, nf, hbm, outs, bufs):
+        self.nl, self.nf = nl, nf
+        self.x, self.y, self.wo_h, self.wi_h = hbm
         self.h_o, self.z_o, self.q_o, self.loss = outs
-        self.h, self.yb, self.a, self.zt, self.wi, self.wo, self.hsem, self.zsem, self.ysem = bufs
-        self.dff = self.a.shape[1]
+        self.h, self.yb, self.acc, self.a, self.z, self.wo, self.wi, self.hsem, self.zsem, self.wsem = bufs
 
     @staticmethod
-    def scratch(tok, dff):
-        return [scratch(BF, tok, D), scratch(BF, tok, D), scratch(BF, RT, dff), scratch(BF, 2, RT, dff),
-                scratch(BF, 2, D, dff), scratch(BF, 2, dff, D), DMA((tok // RT,)), DMA((2, 2)), DMA((2,))]
-
-    def h_copy(self, r, dst):
-        rows = ds(r * RT, RT)
-        return local(self.h.at[rows], dst.at[rows], self.hsem.at[r])
-
-    def prologue(self):
-        self.cy = local(self.y, self.yb, self.ysem.at[1])
-        cx = local(self.x, self.h, self.ysem.at[0])
-        cx.start()
-        self.cy.start()
-        self.loss[...] = jnp.zeros_like(self.loss)
-        cx.wait()
-        for r in range(self.nt):
-            self.h_copy(r, self.h_o.at[0]).start()
-
-    def z_copy(self, li, r, i, slot):
-        c = pl.ds(i * (self.dff // 2), self.dff // 2)
-        return local(self.zt.at[slot, :, c], self.z_o.at[li, ds(r * RT, RT), c], self.zsem.at[slot, i])
-
-    def z_unit(self, li, r, w, i):
-        slot = rem(li * self.nt + r, 2)
-        when(li * self.nt + r > 1)(lambda: self.z_copy(0, 0, i, slot).wait())
-        h = self.h[ds(r * RT, RT)]
-        per = self.dff // D // 2
-        for b in range(i * per, i * per + per):
-            c = pl.ds(b * D, D)
-            z = dg(h, self.wi[w, :, c], 1, 0).astype(BF)
-            self.zt[slot, :, c] = z
-            self.a[:, c] = gelu(z.astype(F32)).astype(BF)
-        self.z_copy(li, r, i, slot).start()
-
-    def h_unit(self, li, r, w, i):
-        rows, c = ds(r * RT, RT), pl.ds(i * BLK, BLK)
-        hn = (self.h[rows, c].astype(F32) + dg(self.a[...], self.wo[w, :, c], 1, 0)).astype(BF)
-        if i == 0:
-            self.h_copy(r, self.h_o.at[0]).wait()
-
-        @when(li < self.nl - 1)
-        def _():
-            self.h[rows, c] = hn
-            if i:
-                self.h_copy(r, self.h_o.at[li + 1]).start()
-
-        @when(li == self.nl - 1)
-        def _():
-            if i == 0:
-                when(r == 0)(self.cy.wait)
-            err = hn.astype(F32) - self.yb[rows, c].astype(F32)
-            self.h[rows, c] = err.astype(BF)
-            if i:
-                self.h_copy(r, self.q_o).start()
-            sq = jnp.sum((err * err).reshape(RT // SUB, SUB, BLK), axis=0)
-            for b in range(BLK // LANE):
-                self.loss[...] += sq[:, b * LANE : (b + 1) * LANE]
-
-    def unit(self, k):
-        return functools.partial(self.h_unit if k // 2 else self.z_unit, i=k % 2)
-
-    def epilogue(self):
-        for slot in TWO:
-            for i in TWO:
-                self.z_copy(0, 0, i, slot).wait()
-        for r in range(self.nt):
-            self.h_copy(r, self.q_o).wait()
+    def scratch(tok, wdt):
+        return [scratch(BF, tok, D), scratch(BF, tok, D), scratch(F32, tok, D), scratch(BF, tok, BLK), scratch(BF, 2, tok, BLK),
+                scratch(wdt, 2, BLK, D), scratch(wdt, 2, D, BLK), DMA((3,)), DMA((2,)), DMA((2, 2))]
 
     @staticmethod
     def shapes(nl, tok, dff):
         S = jax.ShapeDtypeStruct
         return [S((nl, tok, D), BF), S((nl, tok, dff), BF), S((tok, D), BF), S((SUB, LANE), F32)]
 
-
-def forward_kernel(nl, tok, x, y, w_out, w_in, h_o, z_o, q_o, loss, wi32, wo32, wsem, *bufs):
-    fw = Forward(nl, tok, (x, y), (h_o, z_o, q_o, loss), bufs)
-    shares = [(ds(r * (m.shape[1] // fw.nt), m.shape[1] // fw.nt), m, v, w) for m, v, w in ((w_in, wi32, fw.wi), (w_out, wo32, fw.wo)) for r in range(fw.nt)]
-
-    def loads(li, r):
-        return [local(m.at[li, rows], v.at[rows], wsem.at[r, i]) for i, (rows, m, v, _) in enumerate(shares[r :: fw.nt])]
-
-    def take(li, r, last):
-        if not last:
-            wait(loads(li, r))
-        for rows, _, v, w in shares[r :: fw.nt]:
-            w[rem(li, 2), rows] = v[rows].astype(BF)
-        when(li + 1 < nl)(lambda: start(loads(li + 1, r)))
-
-    for r in range(fw.nt):
-        start(loads(0, r))
+    def tiles(self):
+        return [pl.ds(r, FT) for r in range(0, self.h.shape[0], FT)]
+
+    def h_copy(self, dst):
+        return local(self.h, dst, self.hsem.at[0])
+
+    def z_copy(self, s):
+        b = rem(s, 2)
+        return local(self.z.at[b], self.z_o.at[s // self.nf, :, cols(rem(s, self.nf))], self.zsem.at[b])
+
+    def loads(self, s):
+        li, f, b = s // self.nf, rem(s, self.nf), rem(s, 2)
+        return [local(self.wo_h.at[li, cols(f)], self.wo.at[b], self.wsem.at[0, b]),
+                local(self.wi_h.at[li, :, cols(f)], self.wi.at[b], self.wsem.at[1, b])]
+
+    def prologue(self):
+        self.cy = local(self.y, self.yb, self.hsem.at[2])
+        cx = local(self.x, self.h, self.hsem.at[1])
+        start([cx, self.cy])
+        self.loss[...] = jnp.zeros_like(self.loss)
+        cx.wait()
+        self.acc[...] = self.h[...].astype(F32)
+        self.h_copy(self.h_o.at[0]).start()
+
+    def block(self, s):
+        li, f, b = s // self.nf, rem(s, self.nf), rem(s, 2)
+        wait(self.loads(s))
+        when(s > 1)(lambda: self.z_copy(s).wait())
+        wi, wo = self.wi[b].astype(BF), self.wo[b].astype(BF)
+        for rows in self.tiles():
+            z = dg(self.h[rows], wi, 1, 0).astype(BF)
+            self.z[b, rows] = z
+            self.a[rows] = gelu(z.astype(F32)).astype(BF)
+        self.z_copy(s).start()
+        for rows in self.tiles():
+            self.acc[rows] = self.acc[rows] + dg(self.a[rows], wo, 1, 0)
+
+        @when(f == self.nf - 1)
+        def _():
+            self.h_copy(self.h_o.at[0]).wait()
+            step = PC * 7
+
+            @when(li < self.nl - 1)
+            def _():
+                for r in range(0, self.h.shape[0], step):
+                    h = self.acc[r : r + step].astype(BF)
+                    self.h[r : r + step] = h
+                    self.acc[r : r + step] = h.astype(F32)
+                self.h_copy(self.h_o.at[li + 1]).start()
+
+            @when(li == self.nl - 1)
+            def _():
+                self.cy.wait()
+                for r in range(0, self.h.shape[0], step):
+                    err = self.acc[r : r + step].astype(BF).astype(F32) - self.yb[r : r + step].astype(F32)
+                    self.h[r : r + step] = err.astype(BF)
+                    sq = jnp.sum((err * err).reshape(step // SUB, SUB, D), axis=0)
+                    for b in range(D // LANE):
+                        self.loss[...] += sq[:, b * LANE : (b + 1) * LANE]
+                self.h_copy(self.q_o).start()
+
+    def epilogue(self):
+        wait([self.z_copy(s) for s in TWO] + [self.h_copy(self.q_o)])
+
+
+def forward_kernel(nl, x, y, w_out, w_in, h_o, z_o, q_o, loss, *bufs):
+    n = nl * w_out.shape[1] // BLK
+    fw = Forward(nl, n // nl, (x, y, w_out, w_in), (h_o, z_o, q_o, loss), bufs)
+    start(fw.loads(0))
     fw.prologue()
-    for r in range(fw.nt):
-        take(0, r, False)
-
-    def body(li, _):
-        for r in range(fw.nt):
-            when(li + 1 < nl)(lambda: wait(loads(li + 1, r)))
-            take(li + 1, r, True)
-            for k in range(UNITS):
-                fw.unit(k)(li, r, rem(li, 2))
+
+    def body(s, _):
+        when(s + 1 < n)(lambda: start(fw.loads(s + 1)))
+        fw.block(s)
         return 0
 
-    lax.fori_loop(0, nl, body, 0)
+    lax.fori_loop(0, n, body, 0)
     fw.epilogue()
 
 
@@ -542,66 +523,52 @@
     nl, dff, _ = w_out.shape
     tok = x.shape[0]
     return pl.pallas_call(
-        functools.partial(forward_kernel, nl, tok),
+        functools.partial(forward_kernel, nl),
         out_shape=Forward.shapes(nl, tok, dff),
         in_specs=[HBM] * 4,
         out_specs=[HBM] * 3 + [VM],
-        scratch_shapes=[scratch(F32, D, dff), scratch(F32, dff, D), DMA((tok // RT, 2))] + Forward.scratch(tok, dff),
-        compiler_params=pltpu.CompilerParams(vmem_limit_bytes=56 * MIB),
+        scratch_shapes=Forward.scratch(tok, F32),
+        compiler_params=pltpu.CompilerParams(vmem_limit_bytes=63 * MIB),
         name="forward",
     )(x, y, w_out, w_in)
 
 
-def gather_forward_kernel(nl, tok, lags, pe_o, pe_i, x, y, wo_o, wi_o, h_o, z_o, q_o, loss, own_o, own_i, wsem, *bufs):
+def gather_forward_kernel(nl, lags, pe_o, pe_i, x, y, wo_o, wi_o, h_o, z_o, q_o, loss, own_o, own_i, wsem, *bufs):
     g = Geo()
     n = pe_o.shape[0]
     nf = n // nl
     ga = Gather(g, n, nf, lambda q: q, lags, (own_o, own_i), (wo_o, wi_o), bufs[:3])
-    fw = Forward(nl, tok, (x, y), (h_o, z_o, q_o, loss), bufs[3:])
+    fw = Forward(nl, nf, (x, y, wo_o, wi_o), (h_o, z_o, q_o, loss), bufs[3:])
     pieces = [local(src, dst, wsem.at[i]) for i, (src, dst) in enumerate(((pe_o, own_o), (pe_i, own_i)))]
     start(pieces)
-    loads = lambda li: [local(wi_o.at[li], fw.wi.at[rem(li, 2)], wsem.at[0]), local(wo_o.at[li], fw.wo.at[rem(li, 2)], wsem.at[1])]
     fw.prologue()
     g.enter()
     wait(pieces)
-    lead = (ga.mu3 + 1) // 2 + nf
+    lead = (ga.mu3 + 1) // 2 + 2
 
     def body(s, _):
         ga.due(s, 0)
-        u = s - lead
-        up = jnp.maximum(u, 0)
-        li, i = up // nf, rem(up, nf)
-
-        @when(both(u >= 0, i == 0))
-        def _():
-            wait(loads(li))
-
-        for k in range(UNITS):
-            when(both(u >= 0, i < fw.nt * UNITS, rem(i, UNITS) == k))(lambda: fw.unit(k)(li, i // UNITS, rem(li, 2)))
+        when(both(s + 1 >= lead, s + 1 < lead + n))(lambda: start(fw.loads(s + 1 - lead)))
+        when(s >= lead)(lambda: fw.block(s - lead))
         ga.due(s, 1)
-
-        @when(both(u + 1 >= 0, rem(u + 1 + n, nf) == 0, u + 1 < n))
-        def _():
-            start(loads((u + 1) // nf))
-
         return 0
 
     lax.fori_loop(0, lead + n, body, 0)
     fw.epilogue()
 
 
-def gather_forward(pe_o, pe_i, x, y, nl, ns=4, lags=(4, 4, 4, 2), cid=2):
+def gather_forward(pe_o, pe_i, x, y, nl, ns=12, lags=(4, 4, 4, 3), cid=2):
     n, tok = pe_o.shape[0], x.shape[0]
     dff = n // nl * BLK
     S = jax.ShapeDtypeStruct
     return pl.pallas_call(
-        functools.partial(gather_forward_kernel, nl, tok, lags),
+        functools.partial(gather_forward_kernel, nl, lags),
         out_shape=[S((nl, dff, D), BF), S((nl, D, dff), BF)] + Forward.shapes(nl, tok, dff),
         in_specs=[HBM] * 4,
         out_specs=[HBM] * 5 + [VM],
-        scratch_shapes=[scratch(BF, n, 2, PC, BLK)] * 2 + [DMA((2,))] + Gather.scratch(n, ns) + Forward.scratch(tok, dff),
+        scratch_shapes=[scratch(BF, n, 2, PC, BLK)] * 2 + [DMA((2,))] + Gather.scratch(n, ns) + Forward.scratch(tok, BF),
         cost_estimate=pl.CostEstimate(flops=tok * D * dff * nl * 4, bytes_accessed=60 * MIB, transcendentals=0),
-        compiler_params=pltpu.CompilerParams(collective_id=cid, has_side_effects=True, vmem_limit_bytes=48 * MIB),
+        compiler_params=pltpu.CompilerParams(collective_id=cid, has_side_effects=True, vmem_limit_bytes=63 * MIB),
         name="gather_forward",
     )(pe_o, pe_i, x, y)
 
@@ -778,7 +745,7 @@
         wait(copies)
 
 
-def backward(q, h, z, wo, wi, scale, coef, new=None, ns=4, nsl=10, lags=(1, 4, 2, 4), glags=(4, 4, 4, 2), cid=1):
+def backward(q, h, z, wo, wi, scale, coef, new=None, ns=4, nsl=12, lags=(1, 4, 4, 4), glags=(4, 4, 4, 3), ngs=12, cid=1):
     nl, tok, dff = z.shape
     n = nl * dff // BLK
     norm = new is None
@@ -789,7 +756,7 @@
         scr += [piece(F32)] * 2 + [piece(BF)] * 2 + [scratch(F32, PC, BLK)] + PairSum.scratch(4)
         outs, specs, more = [S((n, 2, PC, BLK), BF)] * 2, [HBM] * 2, ()
     else:
-        scr += PairSum.scratch(5) + Gather.scratch(n, ns)
+        scr += PairSum.scratch(5) + Gather.scratch(n, ngs)
         outs, specs, more = [S(new[0].shape, F32), S(new[1].shape, F32), S((SUB, LANE), F32)], [HBM] * 2 + [VM], new
     return pl.pallas_call(
         functools.partial(backward_kernel, nl, tok, ns, nsl, lags, glags, norm, scale, coef),
@@ -798,7 +765,7 @@
         out_specs=specs,
         scratch_shapes=scr,
         cost_estimate=pl.CostEstimate(flops=tok * D * dff * nl * 8, bytes_accessed=60 * MIB, transcendentals=0),
-        compiler_params=pltpu.CompilerParams(collective_id=cid, has_side_effects=True, vmem_limit_bytes=56 * MIB),
+        compiler_params=pltpu.CompilerParams(collective_id=cid, has_side_effects=True, vmem_limit_bytes=63 * MIB),
         name="backward_norm" if norm else "backward_update",
     )(q, h, z, wo, wi, *more)
 

time: 604 us -> 564 us (0.934)
  Pallas kernels: 567 us -> 530 us
    pallas_call x2, Pallas kernels: 163 us -> 134 us  [the longest x1 87.8 us: gather_forward(): pl.pallas_call(functools.partial(gather_forward_kernel, nl, lags), out_sh...]
    pallas_call x2, Pallas kernels: 404 us -> 396 us  [backward(): pl.pallas_call(functools.partial(backward_kernel, nl, tok, ns, nsl, lags,...]
    unnamed x18 -> x6, local copies, waits for them, and re-layouts: 30.2 us -> 26.4 us
where the time goes in v3:
time: 564 us; the launch traced here: 563 us
  Pallas kernels  530 us (94%)
  local copies, waits for them, and re-layouts  29.1 us (5%)
    pallas_call x2, Pallas kernels, backward(): pl.pallas_call(functools.partial(backward_kernel, nl, tok, ns, nsl, lags,...  396 us
    pallas_call x1, Pallas kernels, gather_forward(): pl.pallas_call(functools.partial(gather_forward_kernel, nl, lags), out_sh...  87.8 us
    pallas_call x1, Pallas kernels, forward(): pl.pallas_call(functools.partial(forward_kernel, nl), out_shape=Forward.s...  45.8 us
    unnamed x6, local copies, waits for them, and re-layouts  26.4 us

profile of v3, /device:TPU:0, one launch (start us, length us, event | category | flops | bytes accessed | tf_op | source)
XLA Modules:
  0.0 562.8 jit_solution(15176972092274223649)
XLA Ops:
  0.6 1.9 copy.9
  2.6 1.3 reshape.12.x
  3.9 1.9 copy.10
  5.8 1.3 reshape.13.y
  7.1 45.8 %forward.1 = (bf16[4,1568,512]{2,1,0:T(8,128)(2,1)}, bf16[4,1568,2048]{2,1,0:T(8,128)(2,1)}, bf16[1568,512]{1,0:T(8,128)(2,1)}, f32[8,128]{1,0:T(8,128)}) custom-call(bf16[1568,512]{1,0:T(8,128)(2,1)} %reshape.12.x, bf16[1568,512]{1,0:T(8,128)(2,1)} %reshape.13.y, f32[4,2048,512]{2,1,0:T(8,128)} %refs_5_.1, f32[4,512,2048]{2,1,0:T(8,128)} %refs_6_.1), custom_call_target="tpu_custom_call" | custom-call | tf_op jit(solution)/shard_map/forward/pallas_call | solution.py:525
  52.9 149.8 %backward_norm.1 = (bf16[32,2,16,256]{3,2,1,0:T(8,128)(2,1)}, bf16[32,2,16,256]{3,2,1,0:T(8,128)(2,1)}) custom-call(bf16[1568,512]{1,0:T(8,128)(2,1)} %get-tuple-element.17.refs_0_, bf16[4,1568,512]{2,1,0:T(8,128)(2,1)} %get-tuple-element.18.refs_1_, bf16[4,1568,2048]{2,1,0:T(8,128)(2,1)} %get-tuple-element.19.refs_2_, f32[4,2048,512]{2,1,0:T(8,128)} %refs_5_.1, ...), custom_call_target="tpu_custom_call" | custom-call | flops 52613349376 | bytes 62914560 | tf_op jit(solution)/shard_map/backward_norm/pallas_call | solution.py:761
  202.7 87.8 %gather_forward.1 = (bf16[4,2048,512]{2,1,0:T(8,128)(2,1)}, bf16[4,512,2048]{2,1,0:T(8,128)(2,1)}, bf16[4,1568,512]{2,1,0:T(8,128)(2,1)}, bf16[4,1568,2048]{2,1,...) custom-call(bf16[32,2,16,256]{3,2,1,0:T(8,128)(2,1)} %get-tuple-element.20.pe_o, ...), custom_call_target="tpu_custom_call" | custom-call | flops 26306674688 | bytes 62914560 | tf_op jit(solution)/shard_map/gather_forward/pallas_call | solution.py:564
  290.5 246.7 %backward_update.1 = (f32[4,2048,512]{2,1,0:T(8,128)}, f32[4,512,2048]{2,1,0:T(8,128)}, f32[8,128]{1,0:T(8,128)}) custom-call(bf16[1568,512]{1,0:T(8,128)(2,1)} %get-tuple-element.22.refs_0_, bf16[4,1568,512]{2,1,0:T(8,128)(2,1)} %get-tuple-element.23.refs_1_, bf16[4,1568,2048]{2,1,0:T(8,128)(2,1)} %get-tuple-element.24.refs_2_, ...), custom_call_target="tpu_custom_call" | custom-call | flops 52613349376 | bytes 62914560 | tf_op jit(solution)/shard_map/backward_update/pallas_call | solution.py:761
  537.2 1.3 reduce_sum.9
  539.1 0.0 copy-start
  539.1 12.7 %copy.13 = f32[4,512,2048]{2,1,0:T(8,128)} copy(f32[4,512,2048]{2,1,0:T(8,128)} %get-tuple-element.34) | data formatting | bytes 33554432
  551.8 3.7 copy-done
  555.5 6.2 %copy.14 = f32[4,2048,512]{2,1,0:T(8,128)} copy(f32[4,2048,512]{2,1,0:T(8,128)S(1)} %copy-done) | data formatting | bytes 33554432
Async XLA Ops:
  539.1 16.4 %copy-start = (f32[4,2048,512]{2,1,0:T(8,128)S(1)}, f32[4,2048,512]{2,1,0:T(8,128)}, u32[]{:S(2)}) copy-start(f32[4,2048,512]{2,1,0:T(8,128)} %get-tuple-element.35) | copy-start | bytes 50331652

commit v4 on v3

v4 whole, which is shorter than its diff:
```python
import functools
import math

import jax
import jax.numpy as jnp
from jax import lax
from jax.experimental import pallas as pl
from jax.experimental.pallas import tpu as pltpu
from jax.sharding import PartitionSpec as P

MESH = pl.DeviceIdType.MESH
F32, BF = jnp.float32, jnp.bfloat16
RHO_FRAC = 0.1
LEARN_RATE = 1.0
D = 512
BLK = 256
PC = 16
FT = 224
BT = 1568
SUB, LANE = 8, 128
NZ = 4
HALF = 0.5
MIB = 2**20
GELU_A = math.sqrt(2.0 / math.pi)
GELU_B = 0.044715
TWO = AB = TYPES = DIRS = (0, 1)
SHAPES = ((BLK, D), (D, BLK))
ANY = pl.BlockSpec(memory_space=pl.ANY)
HBM = pl.BlockSpec(memory_space=pltpu.HBM)
VM = pl.BlockSpec(memory_space=pltpu.VMEM)
DMA = pltpu.SemaphoreType.DMA
rem, div = lax.rem, lax.div
when = pl.when


def both(*conds):
    return functools.reduce(jnp.logical_and, conds)


def ds(start, size):
    return pl.ds(pl.multiple_of(start, SUB), size)


def cols(f):
    return pl.ds(pl.multiple_of(f * BLK, BLK), BLK)


def dg(a, b, ca, cb):
    return lax.dot_general(a, b, (((ca,), (cb,)), ((), ())), preferred_element_type=F32)


def scratch(dtype, *shape):
    return pltpu.VMEM(shape, dtype)


def local(src, dst, sem):
    return pltpu.make_async_copy(src, dst, sem)


def start(copies):
    for c in copies:
        c.start()


def wait(copies):
    for c in copies:
        c.wait()


class Geo:
    def __init__(self):
        me = lax.axis_index("data")
        flip = lambda step: me + step - 2 * step * rem(me // step, 2)
        self.me = me
        self.c, self.x, self.y, self.z = [rem(me // step, n) for step, n in ((1, 2), (2, 2), (4, 2), (8, NZ))]
        self.partner, self.xn, self.yn, self.z1, self.z2 = [flip(1 << k) for k in range(5)]
        self.zm, self.zp = me - 8, me + 8
        self.e = self.z // (NZ - 1)
        self.sink = rem(self.z, NZ - 1) == 0
        self.far = me + 24 - 48 * self.e
        self.w = (self.x, self.y)
        self.w2 = (self.y, self.x)
        self.n1 = (self.xn, self.yn)
        self.n2 = (self.yn, self.xn)

    def place(self, dirn):
        return self.z if dirn else NZ - 1 - self.z

    def greet(self):
        self.bar = pltpu.get_barrier_semaphore()
        hello = lambda dev: pl.semaphore_signal(self.bar, device_id=(dev,), device_id_type=MESH)
        for dev in (self.partner, self.xn, self.yn, self.z2):
            hello(dev)
        when(self.z > 0)(lambda: hello(self.zm))
        when(self.z < NZ - 1)(lambda: hello(self.zp))
        when(self.sink)(lambda: hello(self.far))

    def meet(self):
        pl.semaphore_wait(self.bar, 6)

    def half(self, T, c):
        R = SHAPES[T][0]
        return ds(c * (R // 2), R // 2)

    def part(self, T, ab, w):
        R = SHAPES[T][0]
        return self.c * (R // 2) + ab * (R // 4) + w * (R // 8)

    def zrow(self, T, ab, e):
        return self.part(T, ab, self.w[ab]) + e * (SHAPES[T][0] // 16)

    def fin(self, T, ab, mine):
        row = self.zrow(T, ab, self.e)
        w = self.w2[ab] if mine else 1 - self.w2[ab]
        if T:
            return ds(row + w * PC, PC), slice(None)
        return ds(row, PC), cols(w)


def region(out, T, li, f, rows, col=None):
    if T:
        return out[T].at[li, rows, cols(f)]
    return out[T].at[li, ds(f * BLK + rows.start, rows.size), slice(None) if col is None else col]


def schedule(s, j, lag, T):
    d = j - T - lag
    return None if d % 2 else s + d // 2


def run(k, n, what, T, *more):
    if k is not None:
        when(both(k >= 0, k < n))(functools.partial(what, T, k, *more))


class Scatter:
    FLOWS = FD, F1, F3, FM, FP = range(0, 10, 2)
    CREDITS = CD, C1, C3, CM, CP = range(0, 10, 2)

    def __init__(self, g, n, ns, nsl, lags, bufs, deliver):
        self.g, self.n, self.ns, self.nsl, self.deliver = g, n, ns, nsl, deliver
        self.S, self.rD, self.r1, self.rz, self.r3 = [bufs[2 * i : 2 * i + 2] for i in range(5)]
        self.ssem, self.rsem, self.cred = bufs[10:]
        ld, l1, self.lz, l3 = lags
        self.lam1 = ld
        self.lam2 = ld + l1
        self.lam4 = self.lam2 + (NZ - 1) * self.lz + l3

    @staticmethod
    def scratch(ns, nsl):
        out = []
        for lead, div, div2 in (((nsl,), 1, 1), ((ns,), 2, 1), ((ns, 2), 8, 1), ((ns, 2, 2), 16, 1), ((ns, 2), 0, 0)):
            for R, C in SHAPES:
                out.append(scratch(F32, *lead, *((R // div, C) if div else (PC, BLK))))
        return out + [DMA((2, 10, ns))] * 2 + [pltpu.SemaphoreType.REGULAR((2, 10))]

    def copy(self, T, flow, k, src, dst, dev):
        i = (T, flow, rem(k, self.ns))
        return pltpu.make_async_remote_copy(src, dst, self.ssem.at[i], self.rsem.at[i], device_id=(dev,), device_id_type=MESH)

    def take(self, T, credit, k):
        when(k >= self.ns)(lambda: pl.semaphore_wait(self.cred.at[T, credit]))

    def give(self, T, credit, k, dev):
        when(k + self.ns < self.n)(lambda: pl.semaphore_signal(self.cred.at[T, credit], device_id=(dev,), device_id_type=MESH))

    def slots(self, k):
        return rem(k, self.nsl), rem(k, self.ns)

    def to_core(self, T, k):
        s, q = self.slots(k)
        return self.copy(T, self.FD, k, self.S[T].at[s, self.g.half(T, 1 - self.g.c)], self.rD[T].at[q], self.g.partner)

    def first(self, T, k, ab):
        s, q = self.slots(k)
        rows = ds(self.g.part(T, ab, 1 - self.g.w[ab]), SHAPES[T][0] // 8)
        return self.copy(T, self.F1 + ab, k, self.S[T].at[s, rows], self.r1[T].at[q, ab], self.g.n1[ab])

    def zrows(self, T, ab, e):
        return ds(self.g.zrow(T, ab, e), SHAPES[T][0] // 16)

    def along(self, T, k, dirn, ab):
        s, q = self.slots(k)
        flow = (self.FP if dirn else self.FM) + ab
        src = self.S[T].at[s, self.zrows(T, ab, dirn)]
        return self.copy(T, flow, k, src, self.rz[T].at[q, ab, dirn], self.g.zp if dirn else self.g.zm)

    def last(self, T, k, ab):
        s, q = self.slots(k)
        return self.copy(T, self.F3 + ab, k, self.S[T].at[(s, *self.g.fin(T, ab, False))], self.r3[T].at[q, ab], self.g.n2[ab])

    def add(self, T, k, rows, val):
        s, _ = self.slots(k)
        self.S[T][s, rows] = self.S[T][s, rows] + val

    def begin(self, T, k):
        self.take(T, self.CD, k)
        self.to_core(T, k).start()

    def after_core(self, T, k):
        g = self.g
        self.to_core(T, k).wait()
        self.add(T, k, g.half(T, g.c), self.rD[T][rem(k, self.ns)])
        self.give(T, self.CD, k, g.partner)
        for ab in AB:
            self.take(T, self.C1 + ab, k)
            self.first(T, k, ab).start()

    def after_first(self, T, k):
        g = self.g
        for ab in AB:
            self.first(T, k, ab).wait()
        for ab in AB:
            self.add(T, k, ds(g.part(T, ab, g.w[ab]), SHAPES[T][0] // 8), self.r1[T][rem(k, self.ns), ab])
            self.give(T, self.C1 + ab, k, g.n1[ab])

    def line(self, T, k, dirn):
        g = self.g
        p = g.place(dirn)
        credit = self.CP if dirn else self.CM

        @when(k < self.n)
        def _():
            @when(p > 0)
            def _():
                for ab in AB:
                    self.along(T, k, dirn, ab).wait_recv()
                for ab in AB:
                    self.add(T, k, self.zrows(T, ab, dirn), self.rz[T][rem(k, self.ns), ab, dirn])
                self.give(T, credit, k, g.zm if dirn else g.zp)

            @when(p < NZ - 1)
            def _():
                self.take(T, credit, k)
                for ab in AB:
                    self.along(T, k, dirn, ab).start()

            @when(p == NZ - 1)
            def _():
                for ab in AB:
                    self.take(T, self.C3 + ab, k)
                    self.last(T, k, ab).start()

        @when(both(k > 0, p < NZ - 1))
        def _():
            for ab in AB:
                self.along(T, k - 1, dirn, ab).wait_send()

    def after_last(self, T, k):
        g = self.g

        @when(g.sink)
        def _():
            s, q = self.slots(k)
            for ab in AB:
                self.last(T, k, ab).wait()
            for ab in AB:
                self.deliver(T, k, ab, self.S[T][(s, *g.fin(T, ab, True))] + self.r3[T][q, ab])
                self.give(T, self.C3 + ab, k, g.n2[ab])

    def due(self, s, j):
        for T in TYPES:
            run(schedule(s, j, self.lam4, T), self.n, self.after_last, T)
        for T in TYPES:
            k = schedule(s, j, self.lam2, T)
            run(k, self.n, self.after_first, T)
            if k is not None:
                for dirn in DIRS:
                    run(k - self.g.place(dirn) * (self.lz // 2), self.n + 1, self.line, T, dirn)
        for T in TYPES:
            run(schedule(s, j, self.lam1, T), self.n, self.after_core, T)

    def steps(self):
        return self.n + (self.lam4 + 1) // 2 + 1


class Gather:
    FLOWS = F3, FM, FP, FE0, FE1, FD = range(6)

    def __init__(self, g, n, nf, layer, lags, own, out, sems, start=0, whole=None):
        self.g, self.n, self.nf, self.layer, self.own, self.out, self.whole = g, n, nf, layer, own, out, whole
        self.ssem, self.rsem, self.lsem = sems
        self.ns = self.ssem.shape[-1]
        l3, self.lz, le, ld = lags
        self.mu0 = start
        self.mu1 = start + l3
        self.mu2 = self.mu1 + (NZ - 1) * self.lz + le
        self.mu3 = self.mu2 + ld

    @staticmethod
    def scratch(n, ns):
        return [DMA((2, 6, ns)), DMA((2, 6, n)), DMA((2, 2, ns))]

    def region(self, T, k, rows, col=None):
        return region(self.out, T, self.layer(div(k, self.nf)), rem(k, self.nf), rows, col)

    def rows(self, T, k, row, div):
        return self.region(T, k, ds(row, SHAPES[T][0] // div))

    def copy(self, T, flow, k, src, dst, dev):
        return pltpu.make_async_remote_copy(src, dst, self.ssem.at[T, flow, rem(k, self.ns)], self.rsem.at[T, flow, k],
            device_id=(dev,), device_id_type=MESH)

    def keep(self, T, k, ab):
        rows, col = self.g.fin(T, ab, True)
        return local(self.own[T].at[k, ab], self.region(T, k, rows, col), self.lsem.at[T, ab, rem(k, self.ns)])

    def begin(self, T, k):
        g = self.g

        @when(g.sink)
        def _():
            for ab in AB:
                rows, col = g.fin(T, ab, True)
                self.keep(T, k, ab).start()
                self.copy(T, self.F3, k, self.own[T].at[k, ab], self.region(T, k, rows, col), g.n2[ab]).start()

    def over(self, T, flow, k, ref, send=True, recv=True):
        if send:
            local(ref, ref, self.ssem.at[T, flow, rem(k, self.ns)]).wait()
        if recv:
            local(ref, ref, self.rsem.at[T, flow, k]).wait()

    def line(self, T, k, dirn):
        g = self.g
        p = g.place(dirn)
        e = 1 - dirn
        flow = self.FP if dirn else self.FM
        pair = lambda k: self.rows(T, k, 0, 8)

        @when(k < self.n)
        def _():
            @when(p == 0)
            def _():
                for ab in AB:
                    self.keep(T, k, ab).wait()
                self.over(T, self.F3, k, self.own[T].at[k])

            when(p > 0)(lambda: self.over(T, flow, k, pair(k), send=False))
            parts = [self.rows(T, k, g.zrow(T, ab, e), 16) for ab in AB]

            @when(p < NZ - 1)
            def _():
                for r in parts:
                    self.copy(T, flow, k, r, r, g.zp if dirn else g.zm).start()

            for ab in AB:
                self.copy(T, self.FE0 + e, k, parts[ab], parts[ab], g.n1[ab]).start()

        when(both(k > 0, p < NZ - 1))(lambda: self.over(T, flow, k - 1, pair(k - 1), recv=False))

    def to_core(self, T, k):
        r = self.region(T, k, self.g.half(T, self.g.c))
        return self.copy(T, self.FD, k, r, r, self.g.partner)

    def after_first(self, T, k):
        for e in TWO:
            self.over(T, self.FE0 + e, k, self.rows(T, k, 0, 8))
        self.to_core(T, k).start()

    def done(self, T, k):
        self.to_core(T, k).wait()
        if self.whole:
            self.whole(T, k)

    def due(self, s, j):
        for T in TYPES:
            run(schedule(s, j, self.mu0, T), self.n, self.begin, T)
        for T in TYPES:
            k = schedule(s, j, self.mu1, T)
            if k is not None:
                for dirn in DIRS:
                    run(k - self.g.place(dirn) * (self.lz // 2), self.n + 1, self.line, T, dirn)
        for T in TYPES:
            run(schedule(s, j, self.mu2, T), self.n, self.after_first, T)
            run(schedule(s, j, self.mu3, T), self.n, self.done, T)

    def steps(self):
        return self.n + (self.mu3 + 1) // 2 + 1


class PairSum:
    GAP = 3

    def __init__(self, devs, bufs):
        self.devs = devs
        self.part, self.nbr, self.ssem, self.rsem = bufs

    @staticmethod
    def scratch(n):
        return [scratch(F32, n + 1, SUB, LANE), scratch(F32, n, SUB, LANE), DMA((n,)), DMA((n,))]

    def copy(self, r):
        return pltpu.make_async_remote_copy(self.part.at[r], self.nbr.at[r], self.ssem.at[r], self.rsem.at[r],
            device_id=(self.devs[r],), device_id_type=MESH)

    def finish(self, r):
        self.copy(r).wait()
        self.part[r + 1] = self.part[r] + self.nbr[r]

    def due(self, s):
        for r in range(len(self.devs)):
            when(s == r * self.GAP)(lambda: self.copy(r).start())
            when(s == r * self.GAP + self.GAP - 1)(lambda: self.finish(r))

    def now(self):
        for r in range(len(self.devs)):
            self.copy(r).start()
            self.finish(r)


def gelu(z):
    return z * (HALF + HALF * jnp.tanh(z * (GELU_A + (GELU_A * GELU_B) * (z * z))))


def gelu_parts(z):
    zz = z * z
    half = HALF + HALF * jnp.tanh(z * (GELU_A + (GELU_A * GELU_B) * zz))
    slope = half + (z * (half - half * half)) * (2 * GELU_A + (6 * GELU_A * GELU_B) * zz)
    return z * half, slope


class Weights:
    def __init__(self, mats, bufs):
        self.wo_h, self.wi_h = mats
        self.wo, self.wi, self.sem = bufs

    @staticmethod
    def scratch():
        return [scratch(F32, 2, BLK, D), scratch(F32, 2, D, BLK), DMA((2, 2))]

    def loads(self, li, f, b):
        return [local(self.wo_h.at[li, cols(f)], self.wo.at[b], self.sem.at[0, b]), local(self.wi_h.at[li, :, cols(f)], self.wi.at[b], self.sem.at[1, b])]

    def load(self, *at):
        start(self.loads(*at))

    def ready(self, *at):
        wait(self.loads(*at))

    def w_out(self, li, f, b):
        return self.wo[b].astype(BF)

    def w_in(self, li, f, b):
        return self.wi[b].astype(BF)


class Whole:
    def __init__(self, vo, vi):
        self.vo, self.vi = vo, vi

    def load(self, *at):
        pass

    ready = load

    def w_out(self, li, f, b):
        return self.vo[li, cols(f)]

    def w_in(self, li, f, b):
        return self.vi[li, :, cols(f)]


class Acts:
    def __init__(self, hbm, bufs):
        self.h_o, self.z_o = hbm
        self.h, self.hb, self.acc, self.a, self.p, self.z, self.img, self.loss, self.hsem, self.zsem, self.isem = bufs
        self.nl, self.tok, dff = self.z_o.shape
        self.nf = dff // BLK
        self.n = self.nl * self.nf
        self.small = [pl.ds(r, PC * 7) for r in range(0, self.tok, PC * 7)]

    @staticmethod
    def scratch(images, rows):
        tok = images * rows
        return [scratch(BF, tok, D), scratch(BF, 2, tok, D), scratch(F32, tok, D), scratch(BF, tok, BLK), scratch(BF, tok, BLK),
                scratch(BF, 2, tok, BLK), scratch(BF, images, rows, D), scratch(F32, SUB, LANE), DMA((2,)), DMA((2,)), DMA((2,))]

    def tiles(self, size):
        return [pl.ds(r, size) for r in range(0, self.tok, size)]

    def images(self):
        count, rows, _ = self.img.shape
        return [(i, pl.ds(i * rows, rows)) for i in range(count)]

    def z_rows(self, li, f):
        return self.z_o.at[li, :, cols(f)]


class Forward:
    def __init__(self, acts, x, y, weights):
        self.t, self.x, self.y, self.w = acts, x, y, weights

    def at(self, s):
        return div(s, self.t.nf), rem(s, self.t.nf), rem(s, 2)

    def h_copy(self, li):
        return local(self.t.h, self.t.h_o.at[li], self.t.hsem.at[0])

    def z_copy(self, s):
        li, f, b = self.at(s)
        return local(self.t.z.at[b], self.t.z_rows(li, f), self.t.zsem.at[b])

    def image(self, src, i):
        return local(src, self.t.img, self.t.isem.at[i])

    def prologue(self):
        self.image(self.x, 0).start()
        self.w.load(*self.at(0))

    def take_x(self):
        t = self.t
        self.image(self.x, 0).wait()
        for i, rows in t.images():
            t.acc[rows] = t.img[i].astype(F32)
        self.image(self.y, 1).start()
        for rows in t.small:
            t.h[rows] = t.acc[rows].astype(BF)
        self.h_copy(0).start()

    def block(self, s):
        t = self.t
        at = li, f, b = self.at(s)
        self.w.ready(*at)
        when(s + 1 < t.n)(lambda: self.w.load(*self.at(s + 1)))
        when(s > 1)(lambda: self.z_copy(s).wait())
        wi, wo = self.w.w_in(*at), self.w.w_out(*at)
        for rows in t.tiles(FT):
            z = dg(t.h[rows], wi, 1, 0).astype(BF)
            t.z[b, rows] = z
            t.a[rows] = gelu(z.astype(F32)).astype(BF)
        self.z_copy(s).start()
        for rows in t.tiles(FT):
            t.acc[rows] = t.acc[rows] + dg(t.a[rows], wo, 1, 0)
        when(f == t.nf - 1)(functools.partial(self.layer_end, li))

    def layer_end(self, li):
        t = self.t
        self.h_copy(0).wait()

        @when(li < t.nl - 1)
        def _():
            for rows in t.small:
                h = t.acc[rows].astype(BF)
                t.h[rows] = h
                t.acc[rows] = h.astype(F32)
            self.h_copy(li + 1).start()

        @when(li == t.nl - 1)
        def _():
            self.image(self.y, 1).wait()
            for i, rows in t.images():
                t.acc[rows] = t.acc[rows].astype(BF).astype(F32) - t.img[i].astype(F32)
            t.loss[...] = jnp.zeros_like(t.loss)
            for rows in t.small:
                err = t.acc[rows]
                q = err.astype(BF)
                t.h[rows] = q
                t.acc[rows] = q.astype(F32)
                sq = jnp.sum((err * err).reshape(PC * 7 // SUB, SUB, D), axis=0)
                for c in range(0, D, LANE):
                    t.loss[...] += sq[:, c : c + LANE]

    def epilogue(self):
        wait([self.z_copy(s) for s in TWO])


class Backward:
    def __init__(self, acts, weights):
        self.t, self.w = acts, weights

    def at(self, s):
        t = self.t
        return t.nl - 1 - div(s, t.nf), rem(s, t.nf), rem(s, 2)

    def h_load(self, li):
        i = rem(li, 2)
        return local(self.t.h_o.at[li], self.t.hb.at[i], self.t.hsem.at[i])

    def z_load(self, s):
        li, f, b = self.at(s)
        return local(self.t.z_rows(li, f), self.t.z.at[b], self.t.zsem.at[b])

    def load(self, s):
        self.z_load(s).start()
        self.w.load(*self.at(s))

    def prologue(self):
        self.load(0)
        self.h_load(self.t.nl - 1).start()

    def out_block(self, s, dst):
        t = self.t
        at = li, f, b = self.at(s)
        self.z_load(s).wait()
        self.w.ready(*at)
        when(s + 1 < t.n)(lambda: self.load(s + 1))

        @when(f == 0)
        def _():
            self.h_load(li).wait()
            when(li > 0)(lambda: self.h_load(li - 1).start())

        wo = self.w.w_out(*at)
        for rows in t.tiles(BT):
            a, slope = gelu_parts(t.z[b, rows].astype(F32))
            t.a[rows] = a.astype(BF)
            t.p[rows] = (dg(t.h[rows], wo, 1, 1) * slope).astype(BF)
        dst[...] = dg(t.a[...], t.h[...], 0, 0)

    def in_block(self, s, dst):
        t = self.t
        at = li, f, b = self.at(s)
        dst[...] = dg(t.hb[rem(li, 2)], t.p[...], 0, 0)

        @when(li > 0)
        def _():
            wi = self.w.w_in(*at)
            for rows in t.tiles(BT):
                t.acc[rows] = t.acc[rows] + dg(t.p[rows], wi, 1, 1)

            @when(f == t.nf - 1)
            def _():
                for rows in t.small:
                    q = t.acc[rows].astype(BF)
                    t.h[rows] = q
                    t.acc[rows] = q.astype(F32)


class Owned:
    AHEAD = 4

    def __init__(self, g, n, nf, layer, mats, dst, sem):
        self.g, self.n, self.nf, self.layer, self.mats, self.dst, self.sem = g, n, nf, layer, mats, dst, sem

    def due(self, s):
        g = self.g
        sem = self.sem.at[rem(s, self.AHEAD)]

        @when(both(g.sink, s < self.n + self.AHEAD))
        def _():
            @when(s >= self.AHEAD)
            def _():
                for T in TYPES:
                    local(self.dst[T].at[0], self.dst[T].at[0], sem).wait()

            @when(s < self.n)
            def _():
                for T in TYPES:
                    for ab in AB:
                        rows, col = g.fin(T, ab, True)
                        local(region(self.mats, T, self.layer(div(s, self.nf)), rem(s, self.nf), rows, col), self.dst[T].at[s, ab], sem).start()


def step_kernel(ns, nsl, lags, glags, scale, rho, lr, x, y, w_out, w_in, out_o, out_i, loss, h_o, z_o, *refs):
    def take(n):
        nonlocal refs
        mine, refs = refs[:n], refs[n:]
        return mine

    g = Geo()
    g.greet()
    mats = w_out, w_in
    acts = Acts((h_o, z_o), take(11))
    blocks = Weights(mats, take(3))
    whole = vo, vi = take(2)
    sc_bufs, ga_bufs = take(13), take(3)
    own, w_p, pieces = take(2), take(2), take(2)
    sq, wsem = take(2)
    norm = PairSum((g.partner, g.xn, g.yn, g.far), take(4))
    total = PairSum((g.partner, g.xn, g.yn, g.z1, g.z2), take(4))
    n, nf = acts.n, acts.nf
    last_first = lambda q: acts.nl - 1 - q

    fw = Forward(acts, x, y, blocks)
    fw.prologue()
    fw.take_x()

    def forward_step(s, _):
        fw.block(s)
        return 0

    lax.fori_loop(0, n, forward_step, 0)
    fw.epilogue()

    g.meet()
    sq[...] = jnp.zeros_like(sq)
    bw = Backward(acts, blocks)
    bw.prologue()
    owned = Owned(g, n, nf, last_first, mats, w_p, wsem)

    def keep_sums(T, k, ab, val):
        val = val * scale
        own[T][k, ab] = val
        sq[...] += val * val

    def add_up(bw, sc, s, j):
        block = bw.in_block if j else bw.out_block

        @when(s < n)
        def _():
            block(s, sc.S[j].at[rem(s, nsl)])
            sc.begin(j, s)

        sc.due(s, j)

    sc = Scatter(g, n, ns, nsl, lags, sc_bufs, keep_sums)

    def first_sums(s, _):
        owned.due(s)
        for j in TWO:
            add_up(bw, sc, s, j)
        return 0

    lax.fori_loop(0, sc.steps(), first_sums, 0)

    fw = Forward(acts, x, y, Whole(vo, vi))
    fw.prologue()

    @when(g.sink)
    def _():
        quarters = [sq[i * SUB : (i + 1) * SUB, j * LANE : (j + 1) * LANE] for i in TWO for j in TWO]
        norm.part[0] = sum(quarters[1:], quarters[0])
        norm.now()
        sq[...] = jnp.broadcast_to(rho / jnp.sqrt(jnp.broadcast_to(jnp.sum(norm.part[4]), (1, 1))), sq.shape)

    def piece(k):
        of = last_first(div(k, nf)) * nf + rem(k, nf)

        @when(both(g.sink, k < n))
        def _():
            for T in TYPES:
                for ab in AB:
                    pieces[T][k, ab] = (w_p[T][of, ab] + sq[...] * own[T][of, ab]).astype(BF)

    ga = Gather(g, n, nf, lambda q: q, glags, pieces, whole, ga_bufs)
    lead = (ga.mu3 + 1) // 2
    piece(0)

    def gather_step(s, _):
        piece(s + 1)
        ga.due(s, 0)
        when(s == 1)(fw.take_x)
        when(both(s >= lead, s < lead + n))(lambda: fw.block(s - lead))
        ga.due(s, 1)
        return 0

    lax.fori_loop(0, ga.steps(), gather_step, 0)
    fw.epilogue()

    bw2 = Backward(acts, Whole(vo, vi))
    bw2.prologue()
    total.part[0] = acts.loss[...]

    def update(T, k, ab, val):
        w_p[T][k, ab] = w_p[T][k, ab] - lr * (val * scale)

    sc2 = Scatter(g, n, ns, nsl, lags, sc_bufs, update)
    ga2 = Gather(g, n, nf, last_first, glags, w_p, (out_o, out_i), ga_bufs, sc2.lam4 + 1)

    def second_sums(s, _):
        owned.due(s)
        for j in TWO:
            add_up(bw2, sc2, s, j)
            ga2.due(s, j)
        total.due(s)
        return 0

    lax.fori_loop(0, ga2.steps(), second_sums, 0)
    loss[0, 0] = HALF * (jnp.sum(total.part[5]) * scale)


def sam_step(x, y, w_out, w_in, scale, rho, lr, ns=4, nsl=12, lags=(1, 4, 4, 4), glags=(4, 4, 4, 3), ngs=12):
    nl, dff, _ = w_out.shape
    images, rows, _ = x.shape
    tok = images * rows
    n = nl * dff // BLK
    S = jax.ShapeDtypeStruct
    piece = lambda dt: [scratch(dt, n, 2, PC, BLK)] * 2
    bufs = Acts.scratch(images, rows) + Weights.scratch() + [scratch(BF, nl, dff, D), scratch(BF, nl, D, dff)]
    bufs += Scatter.scratch(ns, nsl) + Gather.scratch(n, ngs) + piece(F32) + piece(F32) + piece(BF)
    bufs += [scratch(F32, PC, BLK), DMA((Owned.AHEAD,))] + PairSum.scratch(4) + PairSum.scratch(5)
    return pl.pallas_call(
        functools.partial(step_kernel, ns, nsl, lags, glags, scale, rho, lr),
        out_shape=[S(w_out.shape, F32), S(w_in.shape, F32), S((1, 1), F32), S((nl, tok, D), BF), S((nl, tok, dff), BF)],
        in_specs=[HBM] * 4,
        out_specs=[HBM] * 2 + [pl.BlockSpec(memory_space=pltpu.SMEM)] + [HBM] * 2,
        scratch_shapes=bufs,
        cost_estimate=pl.CostEstimate(flops=tok * D * dff * nl * 24, bytes_accessed=200 * MIB, transcendentals=0),
        compiler_params=pltpu.CompilerParams(collective_id=1, has_side_effects=True, vmem_limit_bytes=67043328),
        name="sam_step",
    )(x, y, w_out, w_in)


def solution(mesh):
    n_dev = mesh.shape["data"]

    def local_step(x_loc, y_loc, w_in, w_out):
        nl, d_model, d_ff = w_in.shape
        scale = 1.0 / (x_loc.shape[0] * n_dev * x_loc.shape[1] * d_model)
        rho = RHO_FRAC * math.sqrt(nl * (d_model + d_ff))
        new_out, new_in, loss, _, _ = sam_step(x_loc, y_loc, w_out, w_in, scale, rho, LEARN_RATE)
        return new_in, new_out, loss.reshape(())

    specs = P("data"), P("data"), P(), P()
    return jax.shard_map(local_step, mesh=mesh, in_specs=specs, out_specs=(P(), P(), P()), check_vma=False)
```

time: 564 us -> 543 us (0.963)
  Pallas kernels: 530 us -> 511 us
    pallas_call x4 -> x1, Pallas kernels: 530 us -> 511 us  [sam_step(): pl.pallas_call(functools.partial(step_kernel, ns, nsl, lags, glags, scale...]
where the time goes in v4:
time: 543 us; the launch traced here: 542 us
  Pallas kernels  511 us (94%)
  local copies, waits for them, and re-layouts  28.8 us (5%)
    pallas_call x1, Pallas kernels, sam_step(): pl.pallas_call(functools.partial(step_kernel, ns, nsl, lags, glags, scale...  511 us
    unnamed x6, local copies, waits for them, and re-layouts  28.8 us

profile of v4, /device:TPU:0, one launch (start us, length us, event | category | flops | bytes accessed | tf_op | source)
XLA Modules:
  0.0 542.2 jit_solution(10337444545094907556)
XLA Ops:
  0.6 3.1 copy.7.x
  3.7 3.1 copy.8.y
  6.8 511.0 %sam_step.1 = (f32[4,2048,512]{2,1,0:T(8,128)}, f32[4,512,2048]{2,1,0:T(8,128)}, f32[1,1]{1,0:T(1,128)}, bf16[4,1568,512]{2,1,0:T(8,128)(2,1)}, bf16[4,1568,2048]{2,1,0:T(8,128)(2,1)}) custom-call(bf16[8,196,512]{2,1,0:T(8,128)(2,1)} %copy.7.x, bf16[8,196,512]{2,1,0:T(8,128)(2,1)} %copy.8.y, f32[4,2048,512]{2,1,0:T(8,128)} %w_out.1, f32[4,512,2048]{2,1,0:T(8,128)} %w_in.1), custom_call_target="tpu_custom_call" | custom-call | flops 157840048128 | bytes 209715200 | tf_op jit(solution)/shard_map/sam_step/pallas_call | solution.py:783
  517.8 0.0 copy-start
  517.8 12.7 %copy.12 = f32[4,512,2048]{2,1,0:T(8,128)} copy(f32[4,512,2048]{2,1,0:T(8,128)} %get-tuple-element.12) | data formatting | bytes 33554432
  530.5 3.7 copy-done
  534.2 6.2 %copy.13 = f32[4,2048,512]{2,1,0:T(8,128)} copy(f32[4,2048,512]{2,1,0:T(8,128)S(1)} %copy-done) | data formatting | bytes 33554432
Async XLA Ops:
  517.8 16.4 %copy-start = (f32[4,2048,512]{2,1,0:T(8,128)S(1)}, f32[4,2048,512]{2,1,0:T(8,128)}, u32[]{:S(2)}) copy-start(f32[4,2048,512]{2,1,0:T(8,128)} %get-tuple-element.13) | copy-start | bytes 50331652

commit v5 on v4

--- a/solution.py
+++ b/solution.py
@@ -77,7 +77,6 @@
         self.zm, self.zp = me - 8, me + 8
         self.e = self.z // (NZ - 1)
         self.sink = rem(self.z, NZ - 1) == 0
-        self.far = me + 24 - 48 * self.e
         self.w = (self.x, self.y)
         self.w2 = (self.y, self.x)
         self.n1 = (self.xn, self.yn)
@@ -93,10 +92,18 @@
             hello(dev)
         when(self.z > 0)(lambda: hello(self.zm))
         when(self.z < NZ - 1)(lambda: hello(self.zp))
-        when(self.sink)(lambda: hello(self.far))
+        known = 1, 2, 4
+        rest = [d for d in range(1, 16) if d not in known]
+        when(self.sink)(lambda: [hello(self.mirror(d)) for d in rest] and None)
+        self.sink_hellos = len(rest)
+
+    def mirror(self, d):
+        flips = (1 - 2 * self.c, 2 - 4 * self.x, 4 - 8 * self.y, 24 - 48 * self.e)
+        return self.me + sum(flip for i, flip in enumerate(flips) if d >> i & 1)
 
     def meet(self):
-        pl.semaphore_wait(self.bar, 6)
+        when(self.sink)(lambda: pl.semaphore_wait(self.bar, 5 + self.sink_hellos))
+        when(jnp.logical_not(self.sink))(lambda: pl.semaphore_wait(self.bar, 6))
 
     def half(self, T, c):
         R = SHAPES[T][0]
@@ -277,8 +284,8 @@
 class Gather:
     FLOWS = F3, FM, FP, FE0, FE1, FD = range(6)
 
-    def __init__(self, g, n, nf, layer, lags, own, out, sems, start=0, whole=None):
-        self.g, self.n, self.nf, self.layer, self.own, self.out, self.whole = g, n, nf, layer, own, out, whole
+    def __init__(self, g, n, nf, layer, lags, own, out, sems, start=0):
+        self.g, self.n, self.nf, self.layer, self.own, self.out = g, n, nf, layer, own, out
         self.ssem, self.rsem, self.lsem = sems
         self.ns = self.ssem.shape[-1]
         l3, self.lz, le, ld = lags
@@ -360,8 +367,6 @@
 
     def done(self, T, k):
         self.to_core(T, k).wait()
-        if self.whole:
-            self.whole(T, k)
 
     def due(self, s, j):
         for T in TYPES:
@@ -403,11 +408,6 @@
             when(s == r * self.GAP)(lambda: self.copy(r).start())
             when(s == r * self.GAP + self.GAP - 1)(lambda: self.finish(r))
 
-    def now(self):
-        for r in range(len(self.devs)):
-            self.copy(r).start()
-            self.finish(r)
-
 
 def gelu(z):
     return z * (HALF + HALF * jnp.tanh(z * (GELU_A + (GELU_A * GELU_B) * (z * z))))
@@ -420,6 +420,9 @@
     return z * half, slope
 
 
+AHEAD = 2
+
+
 class Weights:
     def __init__(self, mats, bufs):
         self.wo_h, self.wi_h = mats
@@ -427,7 +430,7 @@
 
     @staticmethod
     def scratch():
-        return [scratch(F32, 2, BLK, D), scratch(F32, 2, D, BLK), DMA((2, 2))]
+        return [scratch(F32, AHEAD + 1, BLK, D), scratch(F32, AHEAD + 1, D, BLK), DMA((2, AHEAD + 1))]
 
     def loads(self, li, f, b):
         return [local(self.wo_h.at[li, cols(f)], self.wo.at[b], self.sem.at[0, b]), local(self.wi_h.at[li, :, cols(f)], self.wi.at[b], self.sem.at[1, b])]
@@ -464,24 +467,19 @@
 class Acts:
     def __init__(self, hbm, bufs):
         self.h_o, self.z_o = hbm
-        self.h, self.hb, self.acc, self.a, self.p, self.z, self.img, self.loss, self.hsem, self.zsem, self.isem = bufs
+        self.h, self.hb, self.acc, self.a, self.p, self.z, self.y, self.loss, self.hsem, self.zsem, self.isem = bufs
         self.nl, self.tok, dff = self.z_o.shape
         self.nf = dff // BLK
         self.n = self.nl * self.nf
         self.small = [pl.ds(r, PC * 7) for r in range(0, self.tok, PC * 7)]
 
     @staticmethod
-    def scratch(images, rows):
-        tok = images * rows
+    def scratch(tok):
         return [scratch(BF, tok, D), scratch(BF, 2, tok, D), scratch(F32, tok, D), scratch(BF, tok, BLK), scratch(BF, tok, BLK),
-                scratch(BF, 2, tok, BLK), scratch(BF, images, rows, D), scratch(F32, SUB, LANE), DMA((2,)), DMA((2,)), DMA((2,))]
+                scratch(BF, 2, tok, BLK), scratch(BF, tok, D), scratch(F32, SUB, LANE), DMA((2,)), DMA((2,)), DMA((2,))]
 
     def tiles(self, size):
         return [pl.ds(r, size) for r in range(0, self.tok, size)]
-
-    def images(self):
-        count, rows, _ = self.img.shape
-        return [(i, pl.ds(i * rows, rows)) for i in range(count)]
 
     def z_rows(self, li, f):
         return self.z_o.at[li, :, cols(f)]
@@ -492,37 +490,40 @@
         self.t, self.x, self.y, self.w = acts, x, y, weights
 
     def at(self, s):
-        return div(s, self.t.nf), rem(s, self.t.nf), rem(s, 2)
+        return div(s, self.t.nf), rem(s, self.t.nf), rem(s, AHEAD + 1)
 
     def h_copy(self, li):
         return local(self.t.h, self.t.h_o.at[li], self.t.hsem.at[0])
 
     def z_copy(self, s):
-        li, f, b = self.at(s)
+        li, f, _ = self.at(s)
+        b = rem(s, 2)
         return local(self.t.z.at[b], self.t.z_rows(li, f), self.t.zsem.at[b])
 
-    def image(self, src, i):
-        return local(src, self.t.img, self.t.isem.at[i])
+    def x_load(self):
+        return local(self.x, self.t.h, self.t.isem.at[0])
+
+    def y_load(self):
+        return local(self.y, self.t.y, self.t.isem.at[1])
 
     def prologue(self):
-        self.image(self.x, 0).start()
-        self.w.load(*self.at(0))
+        start([self.x_load(), self.y_load()])
+        for s in range(AHEAD):
+            self.w.load(*self.at(s))
 
     def take_x(self):
         t = self.t
-        self.image(self.x, 0).wait()
-        for i, rows in t.images():
-            t.acc[rows] = t.img[i].astype(F32)
-        self.image(self.y, 1).start()
+        self.x_load().wait()
         for rows in t.small:
-            t.h[rows] = t.acc[rows].astype(BF)
+            t.acc[rows] = t.h[rows].astype(F32)
         self.h_copy(0).start()
 
     def block(self, s):
         t = self.t
-        at = li, f, b = self.at(s)
+        at = li, f, _ = self.at(s)
+        b = rem(s, 2)
         self.w.ready(*at)
-        when(s + 1 < t.n)(lambda: self.w.load(*self.at(s + 1)))
+        when(s + AHEAD < t.n)(lambda: self.w.load(*self.at(s + AHEAD)))
         when(s > 1)(lambda: self.z_copy(s).wait())
         wi, wo = self.w.w_in(*at), self.w.w_out(*at)
         for rows in t.tiles(FT):
@@ -548,12 +549,10 @@
 
         @when(li == t.nl - 1)
         def _():
-            self.image(self.y, 1).wait()
-            for i, rows in t.images():
-                t.acc[rows] = t.acc[rows].astype(BF).astype(F32) - t.img[i].astype(F32)
+            self.y_load().wait()
             t.loss[...] = jnp.zeros_like(t.loss)
             for rows in t.small:
-                err = t.acc[rows]
+                err = t.acc[rows].astype(BF).astype(F32) - t.y[rows].astype(F32)
                 q = err.astype(BF)
                 t.h[rows] = q
                 t.acc[rows] = q.astype(F32)
@@ -571,30 +570,31 @@
 
     def at(self, s):
         t = self.t
-        return t.nl - 1 - div(s, t.nf), rem(s, t.nf), rem(s, 2)
+        return t.nl - 1 - div(s, t.nf), rem(s, t.nf), rem(s, AHEAD + 1)
 
     def h_load(self, li):
         i = rem(li, 2)
         return local(self.t.h_o.at[li], self.t.hb.at[i], self.t.hsem.at[i])
 
     def z_load(self, s):
-        li, f, b = self.at(s)
+        li, f, _ = self.at(s)
+        b = rem(s, 2)
         return local(self.t.z_rows(li, f), self.t.z.at[b], self.t.zsem.at[b])
 
-    def load(self, s):
-        self.z_load(s).start()
-        self.w.load(*self.at(s))
-
     def prologue(self):
-        self.load(0)
+        self.z_load(0).start()
+        for s in range(AHEAD):
+            self.w.load(*self.at(s))
         self.h_load(self.t.nl - 1).start()
 
     def out_block(self, s, dst):
         t = self.t
-        at = li, f, b = self.at(s)
+        at = li, f, _ = self.at(s)
+        b = rem(s, 2)
         self.z_load(s).wait()
         self.w.ready(*at)
-        when(s + 1 < t.n)(lambda: self.load(s + 1))
+        when(s + 1 < t.n)(lambda: self.z_load(s + 1).start())
+        when(s + AHEAD < t.n)(lambda: self.w.load(*self.at(s + AHEAD)))
 
         @when(f == 0)
         def _():
@@ -610,7 +610,7 @@
 
     def in_block(self, s, dst):
         t = self.t
-        at = li, f, b = self.at(s)
+        at = li, f, _ = self.at(s)
         dst[...] = dg(t.hb[rem(li, 2)], t.p[...], 0, 0)
 
         @when(li > 0)
@@ -652,7 +652,7 @@
                         local(region(self.mats, T, self.layer(div(s, self.nf)), rem(s, self.nf), rows, col), self.dst[T].at[s, ab], sem).start()
 
 
-def step_kernel(ns, nsl, lags, glags, scale, rho, lr, x, y, w_out, w_in, out_o, out_i, loss, h_o, z_o, *refs):
+def step_kernel(ns, nsl, lags, glags, lags2, glags2, scale, rho, lr, x, y, w_out, w_in, out_o, out_i, loss, h_o, z_o, *refs):
     def take(n):
         nonlocal refs
         mine, refs = refs[:n], refs[n:]
@@ -667,7 +667,7 @@
     sc_bufs, ga_bufs = take(13), take(3)
     own, w_p, pieces = take(2), take(2), take(2)
     sq, wsem = take(2)
-    norm = PairSum((g.partner, g.xn, g.yn, g.far), take(4))
+    shares, ssem, rsem = take(3)
     total = PairSum((g.partner, g.xn, g.yn, g.z1, g.z2), take(4))
     n, nf = acts.n, acts.nf
     last_first = lambda q: acts.nl - 1 - q
@@ -720,9 +720,13 @@
     @when(g.sink)
     def _():
         quarters = [sq[i * SUB : (i + 1) * SUB, j * LANE : (j + 1) * LANE] for i in TWO for j in TWO]
-        norm.part[0] = sum(quarters[1:], quarters[0])
-        norm.now()
-        sq[...] = jnp.broadcast_to(rho / jnp.sqrt(jnp.broadcast_to(jnp.sum(norm.part[4]), (1, 1))), sq.shape)
+        shares[0] = sum(quarters[1:], quarters[0])
+        copies = [pltpu.make_async_remote_copy(shares.at[0], shares.at[d], ssem.at[d], rsem.at[d], device_id=(g.mirror(d),), device_id_type=MESH)
+                  for d in range(1, 16)]
+        start(copies)
+        wait(copies)
+        squares = jnp.sum(jnp.sum(shares[...], axis=0))
+        sq[...] = jnp.broadcast_to(rho / jnp.sqrt(jnp.broadcast_to(squares, (1, 1))), sq.shape)
 
     def piece(k):
         of = last_first(div(k, nf)) * nf + rem(k, nf)
@@ -755,8 +759,8 @@
     def update(T, k, ab, val):
         w_p[T][k, ab] = w_p[T][k, ab] - lr * (val * scale)
 
-    sc2 = Scatter(g, n, ns, nsl, lags, sc_bufs, update)
-    ga2 = Gather(g, n, nf, last_first, glags, w_p, (out_o, out_i), ga_bufs, sc2.lam4 + 1)
+    sc2 = Scatter(g, n, ns, nsl, lags2, sc_bufs, update)
+    ga2 = Gather(g, n, nf, last_first, glags2, w_p, (out_o, out_i), ga_bufs, sc2.lam4 + 1)
 
     def second_sums(s, _):
         owned.due(s)
@@ -770,18 +774,17 @@
     loss[0, 0] = HALF * (jnp.sum(total.part[5]) * scale)
 
 
-def sam_step(x, y, w_out, w_in, scale, rho, lr, ns=4, nsl=12, lags=(1, 4, 4, 4), glags=(4, 4, 4, 3), ngs=12):
+def sam_step(x, y, w_out, w_in, scale, rho, lr, ns=4, nsl=12, lags=(1, 4, 4, 4), glags=(4, 4, 4, 3), lags2=(1, 4, 2, 4), glags2=(4, 4, 4, 3), ngs=12):
     nl, dff, _ = w_out.shape
-    images, rows, _ = x.shape
-    tok = images * rows
+    tok = x.shape[0]
     n = nl * dff // BLK
     S = jax.ShapeDtypeStruct
     piece = lambda dt: [scratch(dt, n, 2, PC, BLK)] * 2
-    bufs = Acts.scratch(images, rows) + Weights.scratch() + [scratch(BF, nl, dff, D), scratch(BF, nl, D, dff)]
+    bufs = Acts.scratch(tok) + Weights.scratch() + [scratch(BF, nl, dff, D), scratch(BF, nl, D, dff)]
     bufs += Scatter.scratch(ns, nsl) + Gather.scratch(n, ngs) + piece(F32) + piece(F32) + piece(BF)
-    bufs += [scratch(F32, PC, BLK), DMA((Owned.AHEAD,))] + PairSum.scratch(4) + PairSum.scratch(5)
+    bufs += [scratch(F32, PC, BLK), DMA((Owned.AHEAD,))] + [scratch(F32, 16, SUB, LANE), DMA((16,)), DMA((16,))] + PairSum.scratch(5)
     return pl.pallas_call(
-        functools.partial(step_kernel, ns, nsl, lags, glags, scale, rho, lr),
+        functools.partial(step_kernel, ns, nsl, lags, glags, lags2, glags2, scale, rho, lr),
         out_shape=[S(w_out.shape, F32), S(w_in.shape, F32), S((1, 1), F32), S((nl, tok, D), BF), S((nl, tok, dff), BF)],
         in_specs=[HBM] * 4,
         out_specs=[HBM] * 2 + [pl.BlockSpec(memory_space=pltpu.SMEM)] + [HBM] * 2,
@@ -799,7 +802,8 @@
         nl, d_model, d_ff = w_in.shape
         scale = 1.0 / (x_loc.shape[0] * n_dev * x_loc.shape[1] * d_model)
         rho = RHO_FRAC * math.sqrt(nl * (d_model + d_ff))
-        new_out, new_in, loss, _, _ = sam_step(x_loc, y_loc, w_out, w_in, scale, rho, LEARN_RATE)
+        x, y = [v.transpose(1, 0, 2).reshape(-1, d_model) for v in (x_loc, y_loc)]
+        new_out, new_in, loss, _, _ = sam_step(x, y, w_out, w_in, scale, rho, LEARN_RATE)
         return new_in, new_out, loss.reshape(())
 
     specs = P("data"), P("data"), P(), P()

time: 543 us -> 529 us (0.974)
  Pallas kernels: 511 us -> 504 us
  local copies, waits for them, and re-layouts: 28.8 us -> 22.6 us
    pallas_call x1, Pallas kernels: 511 us -> 504 us  [sam_step(): pl.pallas_call(functools.partial(step_kernel, ns, nsl, lags, glags, lags2...]
    unnamed x6 -> x4, local copies, waits for them, and re-layouts: 28.8 us -> 22.6 us
where the time goes in v5:
time: 529 us
  Pallas kernels  504 us (95%)
  local copies, waits for them, and re-layouts  22.6 us (4%)
    pallas_call x1, Pallas kernels, sam_step(): pl.pallas_call(functools.partial(step_kernel, ns, nsl, lags, glags, lags2...  504 us
    unnamed x4, local copies, waits for them, and re-layouts  22.6 us

profile of v5, /device:TPU:0, one launch (start us, length us, event | category | flops | bytes accessed | tf_op | source)
XLA Modules:
  0.0 529.2 jit_solution(927327107481248139)
XLA Ops:
  0.6 504.2 %sam_step.1 = (f32[4,2048,512]{2,1,0:T(8,128)}, f32[4,512,2048]{2,1,0:T(8,128)}, f32[1,1]{1,0:T(1,128)}, bf16[4,1568,512]{2,1,0:T(8,128)(2,1)}, bf16[4,1568,2048]{2,1,0:T(8,128)(2,1)}) custom-call(bf16[1568,512]{1,0:T(8,128)(2,1)} %bitcast.7, bf16[1568,512]{1,0:T(8,128)(2,1)} %bitcast.8, f32[4,2048,512]{2,1,0:T(8,128)} %w_out.1, f32[4,512,2048]{2,1,0:T(8,128)} %w_in.1), custom_call_target="tpu_custom_call" | custom-call | flops 157840048128 | bytes 209715200 | tf_op jit(solution)/shard_map/sam_step/pallas_call | solution.py:786
  504.8 0.0 copy-start
  504.8 12.7 %copy.10 = f32[4,512,2048]{2,1,0:T(8,128)} copy(f32[4,512,2048]{2,1,0:T(8,128)} %get-tuple-element.12) | data formatting | bytes 33554432
  517.5 3.7 copy-done
  521.3 6.2 %copy.11 = f32[4,2048,512]{2,1,0:T(8,128)} copy(f32[4,2048,512]{2,1,0:T(8,128)S(1)} %copy-done) | data formatting | bytes 33554432
Async XLA Ops:
  504.8 16.4 %copy-start = (f32[4,2048,512]{2,1,0:T(8,128)S(1)}, f32[4,2048,512]{2,1,0:T(8,128)}, u32[]{:S(2)}) copy-start(f32[4,2048,512]{2,1,0:T(8,128)} %get-tuple-element.13) | copy-start | bytes 50331652

commit v6 on v5

--- a/solution.py
+++ b/solution.py
@@ -19,6 +19,7 @@
 BT = 1568
 SUB, LANE = 8, 128
 NZ = 4
+INSIDE = (1,)
 HALF = 0.5
 MIB = 2**20
 GELU_A = math.sqrt(2.0 / math.pi)
@@ -75,8 +76,12 @@
         self.c, self.x, self.y, self.z = [rem(me // step, n) for step, n in ((1, 2), (2, 2), (4, 2), (8, NZ))]
         self.partner, self.xn, self.yn, self.z1, self.z2 = [flip(1 << k) for k in range(5)]
         self.zm, self.zp = me - 8, me + 8
-        self.e = self.z // (NZ - 1)
+        self.e = self.z // 2
         self.sink = rem(self.z, NZ - 1) == 0
+        self.inner = jnp.logical_not(self.sink)
+        self.outward = self.me + 16 * self.e - 8
+        self.inward = self.me + 8 - 16 * self.e
+        self.across = self.inward
         self.w = (self.x, self.y)
         self.w2 = (self.y, self.x)
         self.n1 = (self.xn, self.yn)
@@ -103,7 +108,7 @@
 
     def meet(self):
         when(self.sink)(lambda: pl.semaphore_wait(self.bar, 5 + self.sink_hellos))
-        when(jnp.logical_not(self.sink))(lambda: pl.semaphore_wait(self.bar, 6))
+        when(self.inner)(lambda: pl.semaphore_wait(self.bar, 6))
 
     def half(self, T, c):
         R = SHAPES[T][0]
@@ -141,13 +146,13 @@
 
 
 class Scatter:
-    FLOWS = FD, F1, F3, FM, FP = range(0, 10, 2)
+    FLOWS = FD, F1, F3, FM, FP, FI = range(0, 12, 2)
     CREDITS = CD, C1, C3, CM, CP = range(0, 10, 2)
 
-    def __init__(self, g, n, ns, nsl, lags, bufs, deliver):
-        self.g, self.n, self.ns, self.nsl, self.deliver = g, n, ns, nsl, deliver
-        self.S, self.rD, self.r1, self.rz, self.r3 = [bufs[2 * i : 2 * i + 2] for i in range(5)]
-        self.ssem, self.rsem, self.cred = bufs[10:]
+    def __init__(self, g, n, ns, nsl, lags, bufs, deliver, inside=()):
+        self.g, self.n, self.ns, self.nsl, self.deliver, self.inside = g, n, ns, nsl, deliver, inside
+        self.S, self.rD, self.r1, self.rz, self.r3, self.ri = [bufs[2 * i : 2 * i + 2] for i in range(6)]
+        self.ssem, self.rsem, self.cred = bufs[12:]
         ld, l1, self.lz, l3 = lags
         self.lam1 = ld
         self.lam2 = ld + l1
@@ -156,10 +161,10 @@
     @staticmethod
     def scratch(ns, nsl):
         out = []
-        for lead, div, div2 in (((nsl,), 1, 1), ((ns,), 2, 1), ((ns, 2), 8, 1), ((ns, 2, 2), 16, 1), ((ns, 2), 0, 0)):
+        for lead, div in (((nsl,), 1), ((ns,), 2), ((ns, 2), 8), ((ns, 2, 2), 16), ((ns, 2), 0), ((ns, 2), 16)):
             for R, C in SHAPES:
                 out.append(scratch(F32, *lead, *((R // div, C) if div else (PC, BLK))))
-        return out + [DMA((2, 10, ns))] * 2 + [pltpu.SemaphoreType.REGULAR((2, 10))]
+        return out + [DMA((2, 12, ns))] * 2 + [pltpu.SemaphoreType.REGULAR((2, 10))]
 
     def copy(self, T, flow, k, src, dst, dev):
         i = (T, flow, rem(k, self.ns))
@@ -253,10 +258,62 @@
             for ab in AB:
                 self.along(T, k - 1, dirn, ab).wait_send()
 
+    def inner_in(self, T, k, e, ab):
+        s, q = self.slots(k)
+        src = self.S[T].at[s, self.zrows(T, ab, e)]
+        return self.copy(T, (self.FP if e else self.FM) + ab, k, src, self.rz[T].at[q, ab, e], self.g.inward)
+
+    def inner_across(self, T, k, ab):
+        s, q = self.slots(k)
+        src = self.S[T].at[s, self.zrows(T, ab, 1 - self.g.e)]
+        return self.copy(T, self.FI + ab, k, src, self.ri[T].at[q, ab], self.g.across)
+
+    def inner_send(self, T, k):
+        every = [(e, ab) for e in DIRS for ab in AB]
+
+        @when(both(self.g.sink, k < self.n))
+        def _():
+            self.take(T, self.CM, k)
+            start([self.inner_in(T, k, e, ab) for e, ab in every])
+
+        @when(both(self.g.sink, k > 0))
+        def _():
+            for e, ab in every:
+                self.inner_in(T, k - 1, e, ab).wait_send()
+
+    def inner_pass(self, T, k):
+        q = rem(k, self.ns)
+
+        @when(both(self.g.inner, k < self.n))
+        def _():
+            for e in DIRS:
+                for ab in AB:
+                    self.inner_in(T, k, e, ab).wait_recv()
+                    self.add(T, k, self.zrows(T, ab, e), self.rz[T][q, ab, e])
+            self.give(T, self.CM, k, self.g.outward)
+            self.take(T, self.CP, k)
+            start([self.inner_across(T, k, ab) for ab in AB])
+
+        @when(both(self.g.inner, k > 0))
+        def _():
+            for ab in AB:
+                self.inner_across(T, k - 1, ab).wait_send()
+
+    def inner_end(self, T, k):
+        @when(self.g.inner)
+        def _():
+            for ab in AB:
+                self.inner_across(T, k, ab).wait_recv()
+                self.add(T, k, self.zrows(T, ab, self.g.e), self.ri[T][rem(k, self.ns), ab])
+            self.give(T, self.CP, k, self.g.across)
+            for ab in AB:
+                self.take(T, self.C3 + ab, k)
+                self.last(T, k, ab).start()
+
     def after_last(self, T, k):
         g = self.g
 
-        @when(g.sink)
+        @when(g.inner if T in self.inside else g.sink)
         def _():
             s, q = self.slots(k)
             for ab in AB:
@@ -271,7 +328,11 @@
         for T in TYPES:
             k = schedule(s, j, self.lam2, T)
             run(k, self.n, self.after_first, T)
-            if k is not None:
+            if T in self.inside:
+                run(k, self.n + 1, self.inner_send, T)
+                run(schedule(s, j, self.lam2 + self.lz, T), self.n + 1, self.inner_pass, T)
+                run(schedule(s, j, self.lam2 + 2 * self.lz, T), self.n, self.inner_end, T)
+            elif k is not None:
                 for dirn in DIRS:
                     run(k - self.g.place(dirn) * (self.lz // 2), self.n + 1, self.line, T, dirn)
         for T in TYPES:
@@ -282,10 +343,11 @@
 
 
 class Gather:
-    FLOWS = F3, FM, FP, FE0, FE1, FD = range(6)
-
-    def __init__(self, g, n, nf, layer, lags, own, out, sems, start=0):
+    FLOWS = F3, FM, FP, FE0, FE1, FD, FO = range(7)
+
+    def __init__(self, g, n, nf, layer, lags, own, out, sems, start=0, inside=()):
         self.g, self.n, self.nf, self.layer, self.own, self.out = g, n, nf, layer, own, out
+        self.inside = inside
         self.ssem, self.rsem, self.lsem = sems
         self.ns = self.ssem.shape[-1]
         l3, self.lz, le, ld = lags
@@ -296,7 +358,7 @@
 
     @staticmethod
     def scratch(n, ns):
-        return [DMA((2, 6, ns)), DMA((2, 6, n)), DMA((2, 2, ns))]
+        return [DMA((2, 7, ns)), DMA((2, 7, n)), DMA((2, 2, ns))]
 
     def region(self, T, k, rows, col=None):
         return region(self.out, T, self.layer(div(k, self.nf)), rem(k, self.nf), rows, col)
@@ -315,7 +377,7 @@
     def begin(self, T, k):
         g = self.g
 
-        @when(g.sink)
+        @when(g.inner if T in self.inside else g.sink)
         def _():
             for ab in AB:
                 rows, col = g.fin(T, ab, True)
@@ -356,6 +418,51 @@
 
         when(both(k > 0, p < NZ - 1))(lambda: self.over(T, flow, k - 1, pair(k - 1), recv=False))
 
+    def pair(self, T, k):
+        return self.rows(T, k, 0, 8)
+
+    def spread(self, T, k, e, *hops):
+        g = self.g
+        parts = [self.rows(T, k, g.zrow(T, ab, e), 16) for ab in AB]
+        for flow, dev in hops:
+            start([self.copy(T, flow, k, r, r, dev) for r in parts])
+        for ab in AB:
+            self.copy(T, self.FE0 + e, k, parts[ab], parts[ab], g.n1[ab]).start()
+
+    def inner_begin(self, T, k):
+        g = self.g
+
+        @when(g.inner)
+        def _():
+            for ab in AB:
+                self.keep(T, k, ab).wait()
+            self.over(T, self.F3, k, self.own[T].at[k])
+            for e in DIRS:
+                when(g.e == e)(lambda: self.spread(T, k, e, (self.FP, g.across), (self.FM, g.outward)))
+
+    def inner_pass(self, T, k):
+        g = self.g
+        for e in DIRS:
+
+            @when(both(g.inner, g.e != e))
+            def _():
+                self.over(T, self.FP, k, self.pair(T, k), send=False)
+                self.spread(T, k, e, (self.FO, g.outward))
+
+            @when(both(g.sink, g.e == e))
+            def _():
+                self.over(T, self.FM, k, self.pair(T, k), send=False)
+                self.spread(T, k, e)
+
+    def inner_end(self, T, k):
+        g = self.g
+        for e in DIRS:
+
+            @when(both(g.sink, g.e != e))
+            def _():
+                self.over(T, self.FO, k, self.pair(T, k), send=False)
+                self.spread(T, k, e)
+
     def to_core(self, T, k):
         r = self.region(T, k, self.g.half(T, self.g.c))
         return self.copy(T, self.FD, k, r, r, self.g.partner)
@@ -367,13 +474,20 @@
 
     def done(self, T, k):
         self.to_core(T, k).wait()
+        if T in self.inside:
+            for flow in (self.FM, self.FP, self.FO):
+                when(self.g.inner)(lambda: self.over(T, flow, k, self.pair(T, k), recv=False))
 
     def due(self, s, j):
         for T in TYPES:
             run(schedule(s, j, self.mu0, T), self.n, self.begin, T)
         for T in TYPES:
             k = schedule(s, j, self.mu1, T)
-            if k is not None:
+            if T in self.inside:
+                run(k, self.n, self.inner_begin, T)
+                run(schedule(s, j, self.mu1 + self.lz, T), self.n, self.inner_pass, T)
+                run(schedule(s, j, self.mu1 + 2 * self.lz, T), self.n, self.inner_end, T)
+            elif k is not None:
                 for dirn in DIRS:
                     run(k - self.g.place(dirn) * (self.lz // 2), self.n + 1, self.line, T, dirn)
         for T in TYPES:
@@ -630,23 +744,20 @@
 class Owned:
     AHEAD = 4
 
-    def __init__(self, g, n, nf, layer, mats, dst, sem):
-        self.g, self.n, self.nf, self.layer, self.mats, self.dst, self.sem = g, n, nf, layer, mats, dst, sem
+    def __init__(self, g, n, nf, layer, mats, dst, sem, inside=()):
+        self.g, self.n, self.nf, self.layer, self.mats, self.dst, self.sem, self.inside = g, n, nf, layer, mats, dst, sem, inside
 
     def due(self, s):
         g = self.g
-        sem = self.sem.at[rem(s, self.AHEAD)]
-
-        @when(both(g.sink, s < self.n + self.AHEAD))
-        def _():
-            @when(s >= self.AHEAD)
+        for T in TYPES:
+            sem = self.sem.at[T, rem(s, self.AHEAD)]
+
+            @when(both(g.inner if T in self.inside else g.sink, s < self.n + self.AHEAD))
             def _():
-                for T in TYPES:
-                    local(self.dst[T].at[0], self.dst[T].at[0], sem).wait()
-
-            @when(s < self.n)
-            def _():
-                for T in TYPES:
+                when(s >= self.AHEAD)(lambda: local(self.dst[T].at[0], self.dst[T].at[0], sem).wait())
+
+                @when(s < self.n)
+                def _():
                     for ab in AB:
                         rows, col = g.fin(T, ab, True)
                         local(region(self.mats, T, self.layer(div(s, self.nf)), rem(s, self.nf), rows, col), self.dst[T].at[s, ab], sem).start()
@@ -664,7 +775,7 @@
     acts = Acts((h_o, z_o), take(11))
     blocks = Weights(mats, take(3))
     whole = vo, vi = take(2)
-    sc_bufs, ga_bufs = take(13), take(3)
+    sc_bufs, ga_bufs = take(15), take(3)
     own, w_p, pieces = take(2), take(2), take(2)
     sq, wsem = take(2)
     shares, ssem, rsem = take(3)
@@ -759,11 +870,12 @@
     def update(T, k, ab, val):
         w_p[T][k, ab] = w_p[T][k, ab] - lr * (val * scale)
 
-    sc2 = Scatter(g, n, ns, nsl, lags2, sc_bufs, update)
-    ga2 = Gather(g, n, nf, last_first, glags2, w_p, (out_o, out_i), ga_bufs, sc2.lam4 + 1)
+    owned2 = Owned(g, n, nf, last_first, mats, w_p, wsem, INSIDE)
+    sc2 = Scatter(g, n, ns, nsl, lags2, sc_bufs, update, INSIDE)
+    ga2 = Gather(g, n, nf, last_first, glags2, w_p, (out_o, out_i), ga_bufs, sc2.lam4 + 1, INSIDE)
 
     def second_sums(s, _):
-        owned.due(s)
+        owned2.due(s)
         for j in TWO:
             add_up(bw2, sc2, s, j)
             ga2.due(s, j)
@@ -774,7 +886,7 @@
     loss[0, 0] = HALF * (jnp.sum(total.part[5]) * scale)
 
 
-def sam_step(x, y, w_out, w_in, scale, rho, lr, ns=4, nsl=12, lags=(1, 4, 4, 4), glags=(4, 4, 4, 3), lags2=(1, 4, 2, 4), glags2=(4, 4, 4, 3), ngs=12):
+def sam_step(x, y, w_out, w_in, scale, rho, lr, ns=4, nsl=12, lags=(1, 4, 4, 4), glags=(4, 4, 4, 3), lags2=(1, 4, 2, 2), glags2=(4, 2, 2, 2), ngs=12):
     nl, dff, _ = w_out.shape
     tok = x.shape[0]
     n = nl * dff // BLK
@@ -782,7 +894,7 @@
     piece = lambda dt: [scratch(dt, n, 2, PC, BLK)] * 2
     bufs = Acts.scratch(tok) + Weights.scratch() + [scratch(BF, nl, dff, D), scratch(BF, nl, D, dff)]
     bufs += Scatter.scratch(ns, nsl) + Gather.scratch(n, ngs) + piece(F32) + piece(F32) + piece(BF)
-    bufs += [scratch(F32, PC, BLK), DMA((Owned.AHEAD,))] + [scratch(F32, 16, SUB, LANE), DMA((16,)), DMA((16,))] + PairSum.scratch(5)
+    bufs += [scratch(F32, PC, BLK), DMA((2, Owned.AHEAD))] + [scratch(F32, 16, SUB, LANE), DMA((16,)), DMA((16,))] + PairSum.scratch(5)
     return pl.pallas_call(
         functools.partial(step_kernel, ns, nsl, lags, glags, lags2, glags2, scale, rho, lr),
         out_shape=[S(w_out.shape, F32), S(w_in.shape, F32), S((1, 1), F32), S((nl, tok, D), BF), S((nl, tok, dff), BF)],

time: 529 us -> 524 us (level)
    pallas_call x1, Pallas kernels: 504 us -> 499 us  [sam_step(): pl.pallas_call(functools.partial(step_kernel, ns, nsl, lags, glags, lags2...]
where the time goes in v6:
time: 524 us
  Pallas kernels  499 us (95%)
  local copies, waits for them, and re-layouts  22.6 us (4%)
    pallas_call x1, Pallas kernels, sam_step(): pl.pallas_call(functools.partial(step_kernel, ns, nsl, lags, glags, lags2...  499 us
    unnamed x4, local copies, waits for them, and re-layouts  22.6 us

profile of v6, /device:TPU:0, one launch (start us, length us, event | category | flops | bytes accessed | tf_op | source)
XLA Modules:
  0.0 523.6 jit_solution(9853712273859465296)
XLA Ops:
  0.6 498.6 %sam_step.1 = (f32[4,2048,512]{2,1,0:T(8,128)}, f32[4,512,2048]{2,1,0:T(8,128)}, f32[1,1]{1,0:T(1,128)}, bf16[4,1568,512]{2,1,0:T(8,128)(2,1)}, bf16[4,1568,2048]{2,1,0:T(8,128)(2,1)}) custom-call(bf16[1568,512]{1,0:T(8,128)(2,1)} %bitcast.7, bf16[1568,512]{1,0:T(8,128)(2,1)} %bitcast.8, f32[4,2048,512]{2,1,0:T(8,128)} %w_out.1, f32[4,512,2048]{2,1,0:T(8,128)} %w_in.1), custom_call_target="tpu_custom_call" | custom-call | flops 157840048128 | bytes 209715200 | tf_op jit(solution)/shard_map/sam_step/pallas_call | solution.py:898
  499.3 0.0 copy-start
  499.3 12.7 %copy.10 = f32[4,512,2048]{2,1,0:T(8,128)} copy(f32[4,512,2048]{2,1,0:T(8,128)} %get-tuple-element.12) | data formatting | bytes 33554432
  511.9 3.7 copy-done
  515.7 6.2 %copy.11 = f32[4,2048,512]{2,1,0:T(8,128)} copy(f32[4,2048,512]{2,1,0:T(8,128)S(1)} %copy-done) | data formatting | bytes 33554432
Async XLA Ops:
  499.3 16.4 %copy-start = (f32[4,2048,512]{2,1,0:T(8,128)S(1)}, f32[4,2048,512]{2,1,0:T(8,128)}, u32[]{:S(2)}) copy-start(f32[4,2048,512]{2,1,0:T(8,128)} %get-tuple-element.13) | copy-start | bytes 50331652

commit v7 on v6

--- a/solution.py
+++ b/solution.py
@@ -645,7 +645,7 @@
             t.z[b, rows] = z
             t.a[rows] = gelu(z.astype(F32)).astype(BF)
         self.z_copy(s).start()
-        for rows in t.tiles(FT):
+        for rows in t.tiles(BT):
             t.acc[rows] = t.acc[rows] + dg(t.a[rows], wo, 1, 0)
         when(f == t.nf - 1)(functools.partial(self.layer_end, li))
 
@@ -794,10 +794,10 @@
     lax.fori_loop(0, n, forward_step, 0)
     fw.epilogue()
 
-    g.meet()
-    sq[...] = jnp.zeros_like(sq)
     bw = Backward(acts, blocks)
     bw.prologue()
+    sq[...] = jnp.zeros_like(sq)
+    g.meet()
     owned = Owned(g, n, nf, last_first, mats, w_p, wsem)
 
     def keep_sums(T, k, ab, val):

time: 524 us -> 522 us (level)
  no operation moved by 1% of the time
where the time goes in v7:
time: 522 us; the launch traced here: 521 us
  Pallas kernels  496 us (95%)
  local copies, waits for them, and re-layouts  22.6 us (4%)
    pallas_call x1, Pallas kernels, sam_step(): pl.pallas_call(functools.partial(step_kernel, ns, nsl, lags, glags, lags2...  496 us
    unnamed x4, local copies, waits for them, and re-layouts  22.6 us

profile of v7, /device:TPU:0, one launch (start us, length us, event | category | flops | bytes accessed | tf_op | source)
XLA Modules:
  0.0 521.4 jit_solution(11819367007003345377)
XLA Ops:
  0.6 496.4 %sam_step.1 = (f32[4,2048,512]{2,1,0:T(8,128)}, f32[4,512,2048]{2,1,0:T(8,128)}, f32[1,1]{1,0:T(1,128)}, bf16[4,1568,512]{2,1,0:T(8,128)(2,1)}, bf16[4,1568,2048]{2,1,0:T(8,128)(2,1)}) custom-call(bf16[1568,512]{1,0:T(8,128)(2,1)} %bitcast.7, bf16[1568,512]{1,0:T(8,128)(2,1)} %bitcast.8, f32[4,2048,512]{2,1,0:T(8,128)} %w_out.1, f32[4,512,2048]{2,1,0:T(8,128)} %w_in.1), custom_call_target="tpu_custom_call" | custom-call | flops 157840048128 | bytes 209715200 | tf_op jit(solution)/shard_map/sam_step/pallas_call | solution.py:898
  497.1 0.0 copy-start
  497.1 12.7 %copy.10 = f32[4,512,2048]{2,1,0:T(8,128)} copy(f32[4,512,2048]{2,1,0:T(8,128)} %get-tuple-element.12) | data formatting | bytes 33554432
  509.8 3.7 copy-done
  513.5 6.2 %copy.11 = f32[4,2048,512]{2,1,0:T(8,128)} copy(f32[4,2048,512]{2,1,0:T(8,128)S(1)} %copy-done) | data formatting | bytes 33554432
Async XLA Ops:
  497.1 16.4 %copy-start = (f32[4,2048,512]{2,1,0:T(8,128)S(1)}, f32[4,2048,512]{2,1,0:T(8,128)}, u32[]{:S(2)}) copy-start(f32[4,2048,512]{2,1,0:T(8,128)} %get-tuple-element.13) | copy-start | bytes 50331652
